TPU v7x, 16 devices: a whole 2x2x2 slice. The times are simulated.
16 devices in a mesh: vp: 2 (over z), dp: 8 (over y, x, core).
Axes of the slice: x: 2, y: 2, z: 2, core: 2. Of those that a mesh axis runs over, the one named last changes fastest.
Arguments:
- hidden: bfloat16 [96, 512, 1024], P('dp')
- mask_pos: int32 [96, 77], P('dp')
- labels: int32 [96, 77], P('dp')
- w_trans: bfloat16 [1024, 1024], replicated
- b_trans: float32 [1024], replicated
- ln_gain: float32 [1024], replicated
- ln_bias: float32 [1024], replicated
- emb_table: bfloat16 [30592, 1024], P('vp')
- b_vocab: float32 [30592], P('vp')
Outputs:
- output 1: float32 [], replicated
- output 2: bfloat16 [96, 512, 1024], P('dp')
- output 3: float32 [1024, 1024], replicated
- output 4: float32 [1024], replicated
- output 5: float32 [1024], replicated
- output 6: float32 [1024], replicated
- output 7: float32 [30592, 1024], P('vp')
- output 8: float32 [30592], P('vp')
All inputs are finite; a program needn't handle non-finite values.
Results may differ from a plain program's by a relative error of at most 0.0107086.
Values sent between devices are 32-bit elements.
A program may use at most 1 GiB of HBM per device.

v0:
```python
import jax
import jax.numpy as jnp
from jax import lax
from jax.sharding import PartitionSpec as P

LN_EPS = 1e-5


def head_norm(pre_act, ln_gain, ln_bias):
    gelu_out = jax.nn.gelu(pre_act, approximate=False)
    row_mean = jnp.mean(gelu_out, axis=-1, keepdims=True)
    centered = gelu_out - row_mean
    row_var = jnp.mean(centered * centered, axis=-1, keepdims=True)
    return centered * lax.rsqrt(row_var + LN_EPS) * ln_gain + ln_bias


def solution(mesh):
    n_groups = mesh.shape["dp"]

    def local_step(hidden, mask_pos, labels, w_trans, b_trans, ln_gain, ln_bias, emb_table, b_vocab):
        n_rows, seq_len = hidden.shape[0], hidden.shape[1]
        n_masks = mask_pos.shape[1]
        shard_rows = emb_table.shape[0]
        n_tokens = n_rows * n_masks * n_groups
        row_start = lax.axis_index("vp") * shard_rows
        pos_onehot = (mask_pos[:, :, None] == jnp.arange(seq_len)[None, None, :]).astype(jnp.bfloat16)
        masked_h = jnp.einsum("clt,cte->cle", pos_onehot, hidden, preferred_element_type=jnp.float32).astype(jnp.bfloat16)
        pre_act = jnp.einsum("cle,ef->clf", masked_h, w_trans, preferred_element_type=jnp.float32) + b_trans
        u_norm, head_vjp = jax.vjp(head_norm, pre_act, ln_gain, ln_bias)
        u_bf16 = u_norm.astype(jnp.bfloat16)
        logits = jnp.einsum("cle,se->cls", u_bf16, emb_table, preferred_element_type=jnp.float32) + b_vocab
        local_max = jnp.max(logits, axis=-1)
        local_sum = jnp.sum(jnp.exp(logits - local_max[..., None]), axis=-1)
        is_label = (labels - row_start)[..., None] == jnp.arange(shard_rows)[None, None, :]
        label_logit = jnp.sum(jnp.where(is_label, logits, 0.0), axis=-1)
        tok_stats = lax.all_gather(jnp.stack([local_max, local_sum, label_logit]), "vp")
        global_max = jnp.max(tok_stats[:, 0], axis=0)
        log_norm = global_max + jnp.log(jnp.sum(tok_stats[:, 1] * jnp.exp(tok_stats[:, 0] - global_max), axis=0))
        target = jnp.sum(tok_stats[:, 2], axis=0)
        mlm_loss = lax.psum(jnp.sum(log_norm - target), "dp") / n_tokens
        d_logits = (jnp.exp(logits - log_norm[..., None]) - is_label.astype(jnp.float32)) / n_tokens
        d_logits_bf = d_logits.astype(jnp.bfloat16)
        d_emb_table = lax.psum(jnp.einsum("cls,cle->se", d_logits_bf, u_bf16, preferred_element_type=jnp.float32), "dp")
        d_b_vocab = lax.psum(jnp.sum(d_logits, axis=(0, 1)), "dp")
        du_part = jnp.einsum("cls,se->cle", d_logits_bf, emb_table, preferred_element_type=jnp.float32).astype(jnp.bfloat16)
        d_unorm = lax.psum(du_part.astype(jnp.float32), "vp")
        d_pre, d_ln_gain, d_ln_bias = head_vjp(d_unorm)
        d_pre_bf = d_pre.astype(jnp.bfloat16)
        d_w_trans = lax.psum(jnp.einsum("cle,clf->ef", masked_h, d_pre_bf, preferred_element_type=jnp.float32), "dp")
        vec_grads = lax.psum(jnp.stack([jnp.sum(d_pre, axis=(0, 1)), d_ln_gain, d_ln_bias]), "dp")
        d_masked = jnp.einsum("clf,ef->cle", d_pre_bf, w_trans, preferred_element_type=jnp.float32).astype(jnp.bfloat16)
        d_hidden = jnp.einsum("clt,cle->cte", pos_onehot, d_masked, preferred_element_type=jnp.float32).astype(jnp.bfloat16)
        return mlm_loss, d_hidden, d_w_trans, vec_grads[0], vec_grads[1], vec_grads[2], d_emb_table, d_b_vocab

    in_specs = (P("dp", None, None), P("dp", None), P("dp", None), P(None, None), P(None), P(None), P(None), P("vp", None), P("vp"))
    out_specs = (P(), P("dp", None, None), P(None, None), P(None), P(None), P(None), P("vp", None), P("vp"))
    return jax.shard_map(local_step, mesh=mesh, in_specs=in_specs, out_specs=out_specs, check_vma=False)
```

profile of v0, /device:TPU:0, one launch (start us, length us, event | category | flops | bytes accessed | tf_op | source)
XLA Modules:
  0.0 1096.8 jit_solution(10512750863395183491)
XLA Ops:
  7.2 7.0 fusion.26
  14.3 3.2 fusion.23
  17.5 10.7 fusion.40
  28.3 1.9 copy-done.1
  30.8 41.5 %add_reduce_fusion = (f32[12,77]{1,0:T(8,128)S(1)}, f32[12,77,15296]{2,1,0:T(8,128)}) fusion(f32[15296]{0:T(1024)S(1)} %copy-done.10, bf16[15296,1024]{1,0:T(8,128)(2,1)} %param.16, f32[12,77,1024]{2,1,0:T(8,128)} %copy-done.1, f32[1024]{0:T(1024)S(1)} %copy-done.18, f32[1024]{0:T(1024)S(1)} %copy-done.13, f32[12,77]{1,0:T(8,128)S(1)} %fusion.36, ...), kind=kOutput, calls=%fused_computation.4 | convolution fusion | flops 28978413568 | bytes 91725392 | tf_op jit(solution)/shard_map/cle,se->cls/dot_general | solution.py:31
  72.3 23.3 %exponential_reduce_fusion = (f32[12,77]{1,0:T(8,128)S(1)}, f32[12,77]{1,0:T(8,128)S(1)}) fusion(f32[12,77,15296]{2,1,0:T(8,128)} %get-tuple-element.32, f32[12,77]{1,0:T(8,128)S(1)} %get-tuple-element.31, f32[15296]{0:T(1024)S(1)} %copy-done.10, s32[12,77]{1,0:T(8,128)S(1)} %broadcast_subtract_fusion), kind=kLoop, calls=%fused_computation.3 | loop fusion | flops 84799168 | bytes 56609984 | tf_op jit(solution)/shard_map/reduce_sum | solution.py:33
  95.7 5.7 all-gather
  101.5 0.6 subtract_reduce_fusion
  102.1 69.3 %convert_convert_fusion = f32[12,77,1024]{2,1,0:T(8,128)} fusion(bf16[15296,1024]{1,0:T(8,128)(2,1)} %param.16, f32[12,77,15296]{2,1,0:T(8,128)} %get-tuple-element.32, f32[12,77]{1,0:T(8,128)S(1)} %get-tuple-element.23, s32[12,77]{1,0:T(8,128)S(1)} %broadcast_subtract_fusion, f32[15296]{0:T(1024)S(1)} %copy-done.10), kind=kOutput, calls=%fused_computation.45 | convolution fusion | flops 29046243328 | bytes 91713504 | tf_op jit(solution)/shard_map/cls,se->cle/dot_general | solution.py:45
  171.4 57.7 %convolution_bitcast_fusion = f32[15296,1024]{1,0:T(8,128)} fusion(f32[12,77,1024]{2,1,0:T(8,128)} %copy-done.1, f32[1024]{0:T(1024)S(1)} %copy-done.18, f32[1024]{0:T(1024)S(1)} %copy-done.13, f32[12,77]{1,0:T(8,128)S(1)} %fusion.36, f32[12,77]{1,0:T(8,128)S(1)} %broadcast_multiply_fusion, f32[12,77,15296]{2,1,0:T(8,128)} %get-tuple-element.32, ...), kind=kOutput, calls=%fused_computation.7 | convolution fusion | flops 29049081856 | bytes 123055296 | tf_op jit(solution)/shard_map/cls,cle->se/dot_general | solution.py:43
  229.1 43.2 %all-reduce.6.cloned.1.call-done = f32[12,77,1024]{2,1,0:T(8,128)} async-done(((f32[12,77,1024]{2,1,0:T(8,128)}), f32[12,77,1024]{2,1,0:T(8,128)}) %all-reduce.6.cloned.1.call-update) | async-done | bytes 3784720 | tf_op jit(solution)/shard_map/psum | solution.py:46
  272.3 4.2 multiply_reduce_fusion.1
  276.7 1.2 copy-done.3
  277.9 2.0 multiply_reduce_fusion
  280.0 1.2 copy-done.6
  281.2 3.3 fusion.39
  284.5 1.3 copy-done.7
  285.8 4.4 convolution_bitcast_fusion.1
  290.3 24.4 %fusion = f32[15296]{0:T(1024)S(1)} fusion(f32[12,77,15296]{2,1,0:T(8,128)} %get-tuple-element.32, f32[12,77]{1,0:T(8,128)S(1)} %get-tuple-element.23, s32[12,77]{1,0:T(8,128)S(1)} %broadcast_subtract_fusion, f32[15296]{0:T(1024)S(1)} %copy-done.10), kind=kLoop, calls=%fused_computation.5 | loop fusion | flops 98919232 | bytes 56663776 | tf_op jit(solution)/shard_map/reduce_sum | solution.py:44
  314.7 28.3 %all-reduce.9 = (f32[]{:T(128)}, f32[3,1024]{1,0:T(4,128)S(1)}, f32[15296]{0:T(1024)}) all-reduce(f32[]{:T(128)} %get-tuple-element.22, f32[3,1024]{1,0:T(4,128)S(1)} %pad_maximum_fusion.1, f32[15296]{0:T(1024)S(1)} %fusion), channel_id=1, replica_groups=mesh['vp'=2,'dp'=8] {'dp'}, use_global_device_ids=true, to_apply=%region_9.10 | all-reduce | flops 18369 | bytes 146952 | tf_op jit(solution)/shard_map/psum | solution.py:40
  344.3 9.7 convolution_convert_fusion
  354.0 687.7 %all-reduce.8.cloned.1.call-done = (f32[1024,1024]{1,0:T(8,128)}, f32[15296,1024]{1,0:T(8,128)}) async-done(((f32[1024,1024]{1,0:T(8,128)}, f32[15296,1024]{1,0:T(8,128)}), (f32[1024,1024]{1,0:T(8,128)}, f32[15296,1024]{1,0:T(8,128)})) %all-reduce.8.cloned.1.call-update) | async-done | bytes 66846736 | tf_op jit(solution)/shard_map/psum | solution.py:49
  1041.8 4.8 copy.26
  1046.5 42.1 %copy.27 = f32[15296,1024]{1,0:T(8,128)} copy(f32[15296,1024]{1,0:T(8,128)} %get-tuple-element.41) | data formatting | bytes 125304832
  (50 shorter events, 1.7 us)
Async XLA Ops:
  7.2 7.1 copy-start
  7.2 265.1 %all-reduce.6.cloned.1.call-start = ((), (), s32[]{:S(2)}) async-start(), calls=%async_computation | async-start | bytes 7864320 | tf_op jit(solution)/shard_map/psum | solution.py:46
  7.2 7.1 copy-start.15
  14.3 3.2 copy-start.8
  17.5 10.7 copy-start.4
  28.2 1.9 copy-start.1
  28.2 2.5 copy-start.17
  28.2 2.6 copy-start.10
  28.2 2.6 copy-start.13
  28.2 2.6 copy-start.18
  30.7 41.6 %copy-start.11 = (f32[12,77]{1,0:T(8,128)}, f32[12,77]{1,0:T(8,128)S(1)}, u32[]{:S(2)}) copy-start(f32[12,77]{1,0:T(8,128)S(1)} %multiply_reduce_fusion.2) | copy-start | bytes 11092
  171.4 870.4 %all-reduce.8.cloned.1.call-start = ((), (), s32[]{:S(2)}) async-start(), calls=%async_computation.1 | async-start | bytes 133693440 | tf_op jit(solution)/shard_map/psum | solution.py:49
  229.1 47.4 %copy-start.12 = (f32[12,77]{1,0:T(8,128)S(1)}, f32[12,77]{1,0:T(8,128)}, u32[]{:S(2)}) copy-start(f32[12,77]{1,0:T(8,128)} %copy-done.11) | copy-start | bytes 11092
  272.3 4.4 copy-start.2
  272.3 5.6 copy-start.3
  277.9 2.1 copy-start.5
  277.9 3.3 copy-start.6
  277.9 3.3 copy-start.16
  281.2 4.6 copy-start.9
  284.5 1.3 copy-start.7
  290.3 54.1 %copy-start.14 = (s32[12,77]{1,0:T(8,128)S(1)}, s32[12,77]{1,0:T(8,128)}, u32[]{:S(2)}) copy-start(s32[12,77]{1,0:T(8,128)} %param.10) | copy-start | bytes 11092
Sparse Core Ops, SparseCore 0:
  171.5 100.7 all-reduce.5
  290.4 751.3 all-reduce.7
where the time goes:
time: 1100 us
  waiting for transfers between devices  731 us (66%)
  matrix products  193 us (18%)
  other arithmetic  69.2 us (6%)
  local copies, waits for them, and re-layouts  53.3 us (5%)
  blocking collectives  34.1 us (3%)
  between operations  16.3 us (1%)
    psum x1, waiting for transfers between devices, local_step(): lax.psum(jnp.einsum('cle,clf->ef', masked_h, d_pre_bf, preferred_element_...  688 us
    dot_general x1, matrix products, local_step(): jnp.einsum('cls,se->cle', d_logits_bf, emb_table, preferred_element_type=...  69.3 us
    dot_general x1, matrix products, local_step(): jnp.einsum('cls,cle->se', d_logits_bf, u_bf16, preferred_element_type=jnp...  57.7 us
    unnamed x40, local copies, waits for them, and re-layouts  52.7 us
    psum x1, waiting for transfers between devices, local_step(): d_unorm = lax.psum(du_part.astype(jnp.float32), 'vp')  43.2 us
    dot_general x1, matrix products, local_step(): jnp.einsum('cle,se->cls', u_bf16, emb_table, preferred_element_type=jnp.f...  41.5 us
    psum x1, blocking collectives, local_step(): mlm_loss = lax.psum(jnp.sum(log_norm - target), 'dp') / n_tokens  28.3 us
    reduce_sum x1, other arithmetic, local_step(): d_b_vocab = lax.psum(jnp.sum(d_logits, axis=(0, 1)), 'dp')  24.4 us
  transfers between devices with their start and end apart: 2, of which 2 were waited for; matrix products, arithmetic and copies ran while one was open for 8% of the time, Pallas kernels for 0%

commit v1 on v0

v1 whole, which is shorter than its diff:
```python
import functools
import math

import jax
import jax.numpy as jnp
from jax import lax
from jax.experimental import pallas as pl
from jax.experimental.pallas import tpu as pltpu
from jax.sharding import PartitionSpec as P


LN_EPS = 1e-5
F32 = jnp.float32
BF16 = jnp.bfloat16
NT = (((1,), (1,)), ((), ()))
LANES = 128
SUBLANES = 16
ROWS = 32
NEGATIVE = -1e30
OWN_V = 512
TILE_V = 768
TILE_T = 512
GATHERED_TILES = 1


def gelu_parts(a):
    cdf = 0.5 * (1.0 + lax.erf(a * math.sqrt(0.5)))
    return cdf, a * cdf


def normalised(g):
    centered = g - jnp.mean(g, axis=-1, keepdims=True)
    scale = lax.rsqrt(jnp.mean(centered * centered, axis=-1, keepdims=True) + LN_EPS)
    return centered * scale, scale


def row_loop(rows, step, body):
    def run(i, carry):
        body(pl.multiple_of(i * step, step))
        return carry

    lax.fori_loop(0, rows // step, run, 0)


def window_start(n_masks, c):
    return pl.multiple_of(n_masks * c // SUBLANES * SUBLANES, SUBLANES)


def head_kernel(n_masks, window, label_at, vp_ref, key_ref, hidden_ref, w_ref, b_ref, gain_ref, beta_ref, label_ref,
                z_ref, pre_ref, u_ref, sent_ref, z_acc, u_acc):
    c = pl.program_id(0)
    slots, seq_len = z_ref.shape[0], hidden_ref.shape[0]
    half = sent_ref.shape[0]

    @pl.when(c == 0)
    def _():
        z_acc[...] = jnp.zeros_like(z_acc)

    here = pl.ds(window_start(n_masks, c), window)
    ids = c * seq_len + lax.broadcasted_iota(jnp.int32, (window, seq_len), 1)
    pick = (key_ref[here, :] == ids).astype(F32).astype(BF16)
    z_acc[here, :] += jnp.dot(pick, hidden_ref[...], preferred_element_type=F32)

    @pl.when(c == pl.num_programs(0) - 1)
    def _():
        z_ref[...] = z_acc[...].astype(BF16)
        pre_ref[...] = jnp.dot(z_ref[...], w_ref[...], preferred_element_type=F32) + b_ref[...]

        def norm(r):
            at = pl.ds(r, ROWS)
            _, g = gelu_parts(pre_ref[at, :])
            xhat, _ = normalised(g)
            u = xhat * gain_ref[...] + beta_ref[...]
            u_acc[at, :] = u
            u_ref[at, :] = u.astype(BF16)

        row_loop(slots, ROWS, norm)
        sent_ref[...] = u_acc[pl.ds(pl.multiple_of(vp_ref[0] * half, SUBLANES), half), :]

        @pl.when(vp_ref[0] == label_at // half)
        def _():
            sent_ref[label_at % half : label_at % half + 1, :] = label_ref[...]


def head(vp, mask_pos, hidden, w, b, gain, beta, label_row, slots, half):
    n_rows, seq_len, width = hidden.shape
    n_masks = mask_pos.shape[1]
    key = (mask_pos + seq_len * jnp.arange(n_rows)[:, None]).reshape(-1, 1)
    key = jnp.pad(key, ((0, slots - n_rows * n_masks), (0, 0)), constant_values=-1)
    whole = lambda rows, cols: pl.BlockSpec((rows, cols), lambda c, v: (0, 0), pipeline_mode=pl.Buffered(1))
    out = lambda rows: pl.BlockSpec((rows, width), lambda c, v: (0, 0), pipeline_mode=pl.Buffered(1))
    return pl.pallas_call(
        functools.partial(head_kernel, n_masks, window_rows(n_masks), n_rows * n_masks),
        name="head",
        grid_spec=pltpu.PrefetchScalarGridSpec(
            num_scalar_prefetch=1,
            grid=(n_rows,),
            in_specs=[whole(slots, 1), pl.BlockSpec((None, seq_len, width), lambda c, v: (c, 0, 0)), whole(width, width)] + [whole(1, width)] * 4,
            out_specs=[out(slots), out(slots), out(slots), out(half)],
            scratch_shapes=[pltpu.VMEM((slots, width), F32), pltpu.VMEM((slots, width), F32)],
        ),
        out_shape=[
            jax.ShapeDtypeStruct((slots, width), BF16),
            jax.ShapeDtypeStruct((slots, width), F32),
            jax.ShapeDtypeStruct((slots, width), BF16),
            jax.ShapeDtypeStruct((half, width), F32),
        ],
        compiler_params=pltpu.CompilerParams(vmem_limit_bytes=50_000_000),
        cost_estimate=pl.CostEstimate(flops=2 * slots * width * width * 4, bytes_accessed=hidden.size * 2, transcendentals=slots * width),
    )(vp, key, hidden, w, b.reshape(1, width), gain.reshape(1, width), beta.reshape(1, width), label_row)


def row_blocks(rows):
    n = 4
    sixteenths = rows // SUBLANES
    sizes = [(sixteenths // n + (i < sixteenths % n)) * SUBLANES for i in range(n)]
    return [slice(sum(sizes[:i]), sum(sizes[: i + 1])) for i in range(n)]


def stats_kernel(emb_ref, bias_ref, u_ref, logit_ref, max_ref, sum_ref, m_acc, l_acc):
    i = pl.program_id(0)

    @pl.when(i == 0)
    def _():
        m_acc[...] = jnp.full_like(m_acc, NEGATIVE)
        l_acc[...] = jnp.zeros_like(l_acc)

    blocks = row_blocks(u_ref.shape[0])

    def logits(rows):
        logit_ref[rows, :] = lax.dot_general(u_ref[rows, :], emb_ref[...], NT, preferred_element_type=F32) + bias_ref[...]

    def stats(rows):
        tiles = [logit_ref[rows, LANES * j : LANES * (j + 1)] for j in range(logit_ref.shape[1] // LANES)]
        old = m_acc[rows, :]
        top = functools.reduce(jnp.maximum, tiles, old)
        l_acc[rows, :] = l_acc[rows, :] * jnp.exp(old - top) + sum(jnp.exp(x - top) for x in tiles)
        m_acc[rows, :] = top

    logits(blocks[0])
    for before, rows in zip(blocks, blocks[1:]):
        logits(rows)
        stats(before)
    stats(blocks[-1])

    @pl.when(i == pl.num_programs(0) - 1)
    def _():
        top = jnp.max(m_acc[...], axis=-1, keepdims=True)
        max_ref[...] = top
        sum_ref[...] = jnp.sum(l_acc[...] * jnp.exp(m_acc[...] - top), axis=-1, keepdims=True)


def tile_of_rows(shard_rows, width):
    last = shard_rows - OWN_V
    return pl.BlockSpec((pl.Element(OWN_V), pl.Element(width)), lambda i: (pl.multiple_of(jnp.minimum(i * OWN_V, last), SUBLANES), 0))


def in_tiles(row, fill):
    n = row.shape[0]
    full = n // OWN_V
    again = OWN_V - n % OWN_V
    last = jnp.concatenate([jnp.full((again,), fill, row.dtype), row[full * OWN_V :]])
    return jnp.concatenate([row[: full * OWN_V], last]).reshape(full + 1, 1, OWN_V)


def own_stats(u, emb, bias):
    slots, width = u.shape
    bias = in_tiles(bias, NEGATIVE)
    n = bias.shape[0]
    col = pl.BlockSpec((slots, 1), lambda i: (0, 0))
    return pl.pallas_call(
        stats_kernel,
        name="own_stats",
        grid=(n,),
        in_specs=[
            tile_of_rows(emb.shape[0], width),
            pl.BlockSpec((None, 1, OWN_V), lambda i: (i, 0, 0)),
            pl.BlockSpec((slots, width), lambda i: (0, 0), pipeline_mode=pl.Buffered(1)),
        ],
        out_specs=[pl.BlockSpec((slots, OWN_V), lambda i: (0, i)), col, col],
        out_shape=[jax.ShapeDtypeStruct((slots, n * OWN_V), F32)] + [jax.ShapeDtypeStruct((slots, 1), F32)] * 2,
        scratch_shapes=[pltpu.VMEM((slots, LANES), F32)] * 2,
        compiler_params=pltpu.CompilerParams(vmem_limit_bytes=50_000_000),
        cost_estimate=pl.CostEstimate(flops=2 * slots * n * OWN_V * width, bytes_accessed=slots * n * OWN_V * 4, transcendentals=slots * n * OWN_V),
    )(emb, bias, u)


def du_kernel(inv_n, spare, logit_ref, emb_ref, ids_ref, lse_ref, lab_ref, du_ref, lse_b, lab_b, hit_acc, acc):
    i = pl.program_id(0)
    blocks = row_blocks(lse_ref.shape[0])

    @pl.when(i == 0)
    def _():
        acc[...] = jnp.zeros_like(acc)
        hit_acc[...] = jnp.zeros_like(hit_acc)
        lse_b[...] = jnp.broadcast_to(lse_ref[...], lse_b.shape)
        lab_b[...] = jnp.broadcast_to(lab_ref[...], lab_b.shape)

    def grad(rows):
        parts = []
        hits = hit_acc[rows, :]
        for j in range(logit_ref.shape[1] // LANES):
            cols = slice(LANES * j, LANES * (j + 1))
            x = logit_ref[rows, cols]
            hit = ids_ref[:, cols] == lab_b[rows, :]
            hits = hits + jnp.where(hit, x, 0.0)
            parts.append((jnp.exp(x - lse_b[rows, :]) - jnp.where(hit, inv_n, 0.0)).astype(BF16))
        hit_acc[rows, :] = hits
        return jnp.concatenate(parts, axis=1)

    for rows in blocks:
        acc[rows, :] += jnp.dot(grad(rows), emb_ref[...], preferred_element_type=F32)

    @pl.when(i == pl.num_programs(0) - 1)
    def _():
        du_ref[...] = acc[...].astype(BF16).astype(F32)
        du_ref[spare : spare + 1, :LANES] = jnp.sum(hit_acc[...], axis=0, keepdims=True)


def own_du(logits, emb, lse, labels, inv_n, n_own):
    slots, width = lse.shape[0], emb.shape[1]
    ids = in_tiles(jnp.arange(emb.shape[0], dtype=jnp.int32), 2**30)
    n = ids.shape[0]
    col = pl.BlockSpec((slots, 1), lambda i: (0, 0), pipeline_mode=pl.Buffered(1))
    return pl.pallas_call(
        functools.partial(du_kernel, inv_n, n_own),
        name="own_du",
        grid=(n,),
        in_specs=[
            pl.BlockSpec((slots, OWN_V), lambda i: (0, i)),
            tile_of_rows(emb.shape[0], width),
            pl.BlockSpec((None, 1, OWN_V), lambda i: (i, 0, 0)),
            col,
            col,
        ],
        out_specs=pl.BlockSpec((slots, width), lambda i: (0, 0), pipeline_mode=pl.Buffered(1)),
        out_shape=jax.ShapeDtypeStruct((slots, width), F32),
        scratch_shapes=[pltpu.VMEM((slots, LANES), F32), pltpu.VMEM((slots, LANES), jnp.int32), pltpu.VMEM((slots, LANES), F32), pltpu.VMEM((slots, width), F32)],
        compiler_params=pltpu.CompilerParams(vmem_limit_bytes=50_000_000),
        cost_estimate=pl.CostEstimate(flops=2 * slots * n * OWN_V * width, bytes_accessed=slots * n * OWN_V * 4, transcendentals=slots * n * OWN_V),
    )(logits, emb, ids, lse, labels)


def head_grad_kernel(n_own, n_tokens, du0_ref, du1_ref, pre_ref, z_ref, w_ref, gain_ref, lse_ref, sums_ref, dz_ref, dab_ref, b_acc, g_acc, o_acc):
    slots, width = pre_ref.shape
    for a in (b_acc, g_acc, o_acc):
        a[...] = jnp.zeros_like(a)

    def fold(x):
        return functools.reduce(jnp.add, [x[8 * j : 8 * (j + 1), :] for j in range(ROWS // 8)])

    def body(r):
        at = pl.ds(r, ROWS)
        real = r + lax.broadcasted_iota(jnp.int32, (ROWS, width), 0) < n_own
        du = jnp.where(real, du0_ref[at, :] + du1_ref[at, :], 0.0)
        a = pre_ref[at, :]
        cdf, g = gelu_parts(a)
        xhat, scale = normalised(g)
        dx = du * gain_ref[...]
        mean_dx = jnp.mean(dx, axis=-1, keepdims=True)
        mean_dxx = jnp.mean(dx * xhat, axis=-1, keepdims=True)
        dg = scale * (dx - mean_dx - xhat * mean_dxx)
        da = dg * (cdf + a * (math.sqrt(0.5 / math.pi) * jnp.exp(-0.5 * a * a)))
        b_acc[...] += fold(da)
        g_acc[...] += fold(du * xhat)
        o_acc[...] += fold(du)
        dab_ref[at, :] = da.astype(BF16)

    row_loop(slots, ROWS, body)
    sums_ref[:width, :] = lax.dot_general(z_ref[...], dab_ref[...], (((0,), (0,)), ((), ())), preferred_element_type=F32)
    dz_ref[...] = lax.dot_general(dab_ref[...], w_ref[...], NT, preferred_element_type=F32).astype(BF16)
    real = lax.broadcasted_iota(jnp.int32, (slots, 1), 0) < n_own
    norms = jnp.sum(jnp.where(real, lse_ref[...], 0.0))
    target = jnp.sum(du0_ref[n_own : n_own + 1, :LANES] + du1_ref[n_own : n_own + 1, :LANES])
    rows = lax.broadcasted_iota(jnp.int32, (8, width), 0)
    tail = jnp.where(rows == 3, (norms - target) / n_tokens, 0.0)
    for j, a in enumerate((b_acc, g_acc, o_acc)):
        tail = jnp.where(rows == j, jnp.sum(a[...], axis=0, keepdims=True), tail)
    sums_ref[width:, :] = tail


def head_grad(du0, du1, pre, z, w, gain, lse, n_own, n_tokens):
    slots, width = pre.shape
    vmem = pl.BlockSpec(memory_space=pltpu.VMEM)
    return pl.pallas_call(
        functools.partial(head_grad_kernel, n_own, n_tokens),
        name="head_grad",
        in_specs=[vmem] * 7,
        out_specs=[vmem] * 2,
        out_shape=[jax.ShapeDtypeStruct((width + 8, width), F32), jax.ShapeDtypeStruct((slots, width), BF16)],
        scratch_shapes=[pltpu.VMEM((slots, width), BF16)] + [pltpu.VMEM((8, width), F32)] * 3,
        compiler_params=pltpu.CompilerParams(vmem_limit_bytes=55_000_000),
        cost_estimate=pl.CostEstimate(flops=8 * slots * width * width, bytes_accessed=slots * width * 18, transcendentals=slots * width),
    )(du0, du1, pre, z, w, gain.reshape(1, width), lse)


def window_rows(n_masks):
    return -(-(n_masks + SUBLANES - 1) // SUBLANES) * SUBLANES


def scatter_kernel(n_masks, window, pos_ref, dz_ref, out_ref):
    c = pl.program_id(0)
    seq_len = out_ref.shape[0]
    hit = pos_ref[...] == lax.broadcasted_iota(jnp.int32, (seq_len, window), 0)
    rows = dz_ref[pl.ds(window_start(n_masks, c), window), :]
    out_ref[...] = jnp.dot(hit.astype(F32).astype(BF16), rows, preferred_element_type=F32).astype(BF16)


def scatter(mask_pos, dz, seq_len):
    n_rows, n_masks = mask_pos.shape
    width = dz.shape[1]
    window = window_rows(n_masks)
    lead = [n_masks * c % SUBLANES for c in range(n_rows)]
    pos = jnp.stack([jnp.pad(mask_pos[c], (a, window - n_masks - a), constant_values=-1) for c, a in enumerate(lead)])
    return pl.pallas_call(
        functools.partial(scatter_kernel, n_masks, window),
        name="scatter",
        grid=(n_rows,),
        in_specs=[pl.BlockSpec((None, 1, window), lambda c: (c, 0, 0)), pl.BlockSpec(dz.shape, lambda c: (0, 0), pipeline_mode=pl.Buffered(1))],
        out_specs=pl.BlockSpec((None, seq_len, width), lambda c: (c, 0, 0)),
        out_shape=jax.ShapeDtypeStruct((n_rows, seq_len, width), BF16),
        cost_estimate=pl.CostEstimate(flops=2 * n_rows * seq_len * window * width, bytes_accessed=n_rows * seq_len * width * 2, transcendentals=0),
    )(pos[:, None, :], dz)


def emb_grad_kernel(tc, n, tail, inv_n, bv, off_ref, lab_ref, lse_ref, emb_ref, bias_ref, u_ref, *rest):
    (*dout_refs, db_ref, s0, s1, bb_ref) = rest
    acc = dout_refs[0]
    row0 = (off_ref[0] + pl.program_id(0)) * bv
    bb_ref[...] = jnp.broadcast_to(bias_ref[...], (bv, LANES))
    db_ref[...] = jnp.zeros_like(db_ref)
    acc[...] = jnp.zeros_like(acc)

    def at(i):
        return i * tc if isinstance(i, int) else pl.multiple_of(i * tc, tc)

    def dot1(t0, w):
        return lax.dot_general(emb_ref[...], u_ref[pl.ds(t0, w), :], NT, preferred_element_type=F32)

    def grad(s_ref, t0, w):
        ids = row0 + lax.broadcasted_iota(jnp.int32, (bv, LANES), 0)
        total = None
        parts = []
        for j in range(w // LANES):
            cols = pl.ds(t0 + LANES * j, LANES)
            x = s_ref[:, LANES * j : LANES * (j + 1)] + bb_ref[...] - lse_ref[:, cols]
            g = jnp.exp(x) - jnp.where(ids == lab_ref[:, cols], inv_n, 0.0)
            total = g if total is None else total + g
            parts.append(g.astype(BF16))
        db_ref[...] += total
        return jnp.concatenate(parts, axis=1)

    def dot2(g, t0, w):
        acc[...] += jnp.dot(g, u_ref[pl.ds(t0, w), :], preferred_element_type=F32)

    s0[...] = dot1(0, tc)

    def body(i, carry):
        a = 2 * i
        s1[...] = dot1(at(a + 1), tc)
        dot2(grad(s0, at(a), tc), at(a), tc)
        s0[...] = dot1(at(a + 2), tc)
        dot2(grad(s1, at(a + 1), tc), at(a + 1), tc)
        return carry

    lax.fori_loop(0, n // 2 - 1, body, 0)
    s1[...] = dot1((n - 1) * tc, tc)
    dot2(grad(s0, (n - 2) * tc, tc), (n - 2) * tc, tc)
    if tail:
        s0[:, :tail] = dot1(n * tc, tail)
    dot2(grad(s1, (n - 1) * tc, tc), (n - 1) * tc, tc)
    if tail:
        dot2(grad(s0, n * tc, tail), n * tc, tail)
    for other in dout_refs[1:]:
        other[...] = acc[...]


def emb_grad(first_tile, n_tiles, place_rows, inv_n, labels, lse, emb, bias, u):
    n_tok, width = u.shape
    n, tail = divmod(n_tok, TILE_T)
    if n % 2:
        n, tail = n - 1, tail + TILE_T
    bv = TILE_V
    rows = n_tiles * bv
    once = pl.Buffered(1)
    out_specs = [pl.BlockSpec((bv, width), lambda i, o: (i, 0)), pl.BlockSpec((bv, LANES), lambda i, o: (i, 0))]
    out_shape = [jax.ShapeDtypeStruct((rows, width), F32), jax.ShapeDtypeStruct((rows, LANES), F32)]
    if place_rows:
        out_specs.insert(1, pl.BlockSpec((bv, width), lambda i, o: (o[0] + i, 0)))
        out_shape.insert(1, jax.ShapeDtypeStruct((place_rows, width), F32))
    grid_spec = pltpu.PrefetchScalarGridSpec(
        num_scalar_prefetch=1,
        grid=(n_tiles,),
        in_specs=[
            pl.BlockSpec((1, n_tok), lambda i, o: (0, 0), pipeline_mode=once),
            pl.BlockSpec((1, n_tok), lambda i, o: (0, 0), pipeline_mode=once),
            pl.BlockSpec((bv, width), lambda i, o: (o[0] + i, 0)),
            pl.BlockSpec((bv, 1), lambda i, o: (o[0] + i, 0)),
            pl.BlockSpec((n_tok, width), lambda i, o: (0, 0), pipeline_mode=once),
        ],
        out_specs=out_specs,
        scratch_shapes=[pltpu.VMEM((bv, TILE_T), F32), pltpu.VMEM((bv, TILE_T), F32), pltpu.VMEM((bv, LANES), F32)],
    )
    flops = 4 * rows * n_tok * width
    return pl.pallas_call(
        functools.partial(emb_grad_kernel, TILE_T, n, tail, inv_n, bv),
        grid_spec=grid_spec,
        out_shape=out_shape,
        compiler_params=pltpu.CompilerParams(vmem_limit_bytes=62_000_000),
        cost_estimate=pl.CostEstimate(flops=flops, bytes_accessed=n_tok * width * 2 + rows * width * 6, transcendentals=rows * n_tok),
    )(first_tile, labels, lse, emb, bias, u)


def round_kernel(src_ref, out_ref):
    out_ref[...] = src_ref[...].astype(out_ref.dtype)


def round_rows(src, block):
    rows, width = src.shape
    return pl.pallas_call(
        round_kernel,
        grid=(rows // block,),
        in_specs=[pl.BlockSpec((block, width), lambda i: (i, 0))],
        out_specs=pl.BlockSpec((block, width), lambda i: (i, 0)),
        out_shape=jax.ShapeDtypeStruct(src.shape, BF16),
        cost_estimate=pl.CostEstimate(flops=rows * width, bytes_accessed=rows * width * 6, transcendentals=0),
    )(src)


def copy_kernel(off_ref, src_ref, full_ref, out_ref):
    out_ref[...] = src_ref[...]


def put_rows(first_tile, src, full, n_src, n_tiles):
    bv, width = TILE_V, full.shape[1]
    return pl.pallas_call(
        copy_kernel,
        grid_spec=pltpu.PrefetchScalarGridSpec(
            num_scalar_prefetch=1,
            grid=(n_src, n_tiles),
            in_specs=[pl.BlockSpec((None, bv, width), lambda d, i, o: (d, i, 0)), pl.BlockSpec(memory_space=pl.ANY)],
            out_specs=pl.BlockSpec((bv, width), lambda d, i, o: (o[0] + d * n_tiles + i, 0)),
        ),
        out_shape=jax.ShapeDtypeStruct(full.shape, full.dtype),
        input_output_aliases={2: 0},
        cost_estimate=pl.CostEstimate(flops=n_src * n_tiles * bv * width, bytes_accessed=n_src * n_tiles * bv * width * 8, transcendentals=0),
    )(first_tile, src, full)


def solution(mesh):
    n_groups, n_vp = mesh.shape["dp"], mesh.shape["vp"]

    def local_step(hidden, mask_pos, labels, w_trans, b_trans, ln_gain, ln_bias, emb_table, b_vocab):
        n_rows, seq_len, width = hidden.shape
        n_masks = mask_pos.shape[1]
        shard_rows = emb_table.shape[0]
        n_own = n_rows * n_masks
        n_tokens = n_own * n_groups
        pad = -n_own % (SUBLANES * n_vp)
        me = lax.axis_index("dp")
        row_start = lax.axis_index("vp") * shard_rows
        vp = lax.axis_index("vp")

        slots = n_own + pad
        half = slots // n_vp
        label_row = jnp.pad(labels.reshape(1, n_own).astype(F32), ((0, 0), (0, width - n_own)), constant_values=-1.0)
        z, pre_act, u_own, sent = head(vp.reshape(1), mask_pos, hidden, w_trans, b_trans, ln_gain, ln_bias, label_row, slots, half)
        gathered = lax.all_gather(sent, ("vp", "dp"), axis=0, tiled=True)
        u_all = round_rows(gathered, slots)

        def token_order(rows):
            return jnp.swapaxes(rows.reshape(n_groups, n_vp, half), 0, 1).reshape(1, -1)

        own_slots = gathered.reshape(n_vp, n_groups, half, width)
        labels_all = token_order(own_slots[n_own // half, :, n_own % half, :slots].astype(jnp.int32) - row_start)

        logits, top, total = own_stats(u_own, emb_table, b_vocab)
        stats = jnp.pad(jnp.concatenate([top, total], axis=1).T, ((0, 0), (0, -slots % 1024))).reshape(-1, LANES)
        stats = lax.all_gather(stats, ("vp", "dp"), axis=0, tiled=True).reshape(n_vp, n_groups, 2, -1)
        top = jnp.max(stats[:, :, 0], axis=0)
        log_norm = top + jnp.log(jnp.sum(stats[:, :, 1] * jnp.exp(stats[:, :, 0] - top), axis=0))
        lse = jnp.where(jnp.arange(log_norm.shape[1]) < n_own, log_norm + math.log(n_tokens), -NEGATIVE)[:, :slots]
        lse_all = token_order(lse)
        lse_own = lax.dynamic_slice_in_dim(lse, me, 1).reshape(slots, 1)
        norm_own = lax.dynamic_slice_in_dim(log_norm, me, 1)[:, :slots].reshape(slots, 1)
        label_col = jnp.pad((labels - row_start).reshape(n_own, 1), ((0, pad), (0, 0)), constant_values=-(2**30))
        du_part = own_du(logits, emb_table, lse_own, label_col, 1.0 / n_tokens, n_own)

        tiles = pl.cdiv(shard_rows, TILE_V)
        k = GATHERED_TILES
        m = (tiles - n_groups * k) // 2
        core = lax.rem(me, 2)
        bias_col = b_vocab.reshape(shard_rows, 1)
        lse_all, du_part = lax.optimization_barrier((lse_all, du_part))
        part1, db1 = emb_grad((me * k).reshape(1), k, 0, 1.0 / n_tokens, labels_all, lse_all, emb_table, bias_col, u_all)
        mine = (n_groups * k + core * m).reshape(1)
        theirs = (n_groups * k + (1 - core) * m).reshape(1)
        rows1 = lax.all_gather(jnp.concatenate([part1, jnp.pad(jnp.pad(jnp.sum(db1, axis=1), (0, -k * TILE_V % width)).reshape(-1, width), ((0, 8 - pl.cdiv(k * TILE_V, width)), (0, 0)))]), "dp", axis=0)
        swap = [(i, i ^ 1) for i in range(n_groups)]
        du_other = lax.ppermute(du_part, "vp", [(0, 1), (1, 0)])
        sum_in, dz = head_grad(du_part, du_other, pre_act, z, w_trans, ln_gain, norm_own, n_own, n_tokens)
        lse_all, sum_in = lax.optimization_barrier((lse_all, sum_in))

        part2, full, db2 = emb_grad(mine, m, shard_rows, 1.0 / n_tokens, labels_all, lse_all, emb_table, bias_col, u_all)
        rows2 = lax.ppermute(part2, "dp", swap)
        db2 = jnp.sum(db2, axis=1)
        db2_other = lax.ppermute(db2, "dp", swap)
        rows1, sum_in = lax.optimization_barrier((rows1, sum_in))
        sums = lax.psum(sum_in, "dp")

        full = put_rows(jnp.zeros((1,), jnp.int32), rows1, full, n_groups, k)
        d_emb_table = put_rows(theirs, rows2[None], full, 1, m)
        db1_all = rows1[:, k * TILE_V :].reshape(n_groups, -1)[:, : k * TILE_V].reshape(-1)
        db_first, db_last = jnp.where(core == 0, db2, db2_other), jnp.where(core == 0, db2_other, db2)
        d_b_vocab = jnp.concatenate([db1_all, db_first, db_last])[:shard_rows]

        d_hidden = scatter(mask_pos, dz, seq_len)
        return sums[width + 3, 0], d_hidden, sums[:width], sums[width], sums[width + 1], sums[width + 2], d_emb_table, d_b_vocab

    in_specs = (P("dp", None, None), P("dp", None), P("dp", None), P(None, None), P(None), P(None), P(None), P("vp", None), P("vp"))
    out_specs = (P(), P("dp", None, None), P(None, None), P(None), P(None), P(None), P("vp", None), P("vp"))

    return jax.shard_map(local_step, mesh=mesh, in_specs=in_specs, out_specs=out_specs, check_vma=False)
```

time: 1100 us -> 590 us (0.54)
  waiting for transfers between devices: 731 us -> 110 us
  Pallas kernels: 0 us -> 413 us
  matrix products: 193 us -> 0 us
  other arithmetic: 69.2 us -> 8.3 us
  local copies, waits for them, and re-layouts: 53.3 us -> 24.3 us
  blocking collectives: 34.1 us -> 15.5 us
    psum x2 -> x1, waiting for transfers between devices: 731 us -> 9.6 us  [local_step(): sums = lax.psum(sum_in, 'dp')]
    pallas_call x0 -> x10, Pallas kernels: none -> 413 us  [the longest x2 201 us: emb_grad(): pl.pallas_call(functools.partial(emb_grad_kernel, TILE_T, n, tail, inv_n,...]
    dot_general x7 -> x0, matrix products: 193 us -> none  [the longest x1 69.3 us: local_step(): jnp.einsum('cls,se->cle', d_logits_bf, emb_table, preferred_element_type=...]
    ppermute x0 -> x3, waiting for transfers between devices: none -> 101 us  [the longest x1 83 us: local_step(): du_other = lax.ppermute(du_part, 'vp', [(0, 1), (1, 0)])]
    reduce_sum x10 -> x3, other arithmetic: 69.1 us -> 1.88 us  [the longest x1 1.17 us: local_step(): jnp.sum(db1, axis=1)]
    unnamed x40 -> x20, local copies, waits for them, and re-layouts: 52.7 us -> 6.88 us
    psum x1 -> x0, blocking collectives: 28.3 us -> none  [local_step(): mlm_loss = lax.psum(jnp.sum(log_norm - target), 'dp') / n_tokens]
  transfers between devices with their start and end apart: 2 -> 6, of which waited for: 2 -> 3; matrix products, arithmetic and copies ran while one was open for 8% -> 2% of each run, Pallas kernels for 0% -> 58%
where the time goes in v1:
time: 590 us; the launch traced here: 587 us
  Pallas kernels  413 us (70%)
  waiting for transfers between devices  110 us (19%)
  local copies, waits for them, and re-layouts  24.3 us (4%)
  blocking collectives  15.5 us (3%)
  between operations  14.1 us (2%)
  other arithmetic  8.3 us (1%)
    pallas_call x2, Pallas kernels, emb_grad(): pl.pallas_call(functools.partial(emb_grad_kernel, TILE_T, n, tail, inv_n,...  201 us
    ppermute x1, waiting for transfers between devices, local_step(): du_other = lax.ppermute(du_part, 'vp', [(0, 1), (1, 0)])  83 us
    pallas_call x1, Pallas kernels, own_stats(): pl.pallas_call(stats_kernel, name='own_stats', grid=(n,), in_specs=[tile_...  56.4 us
    pallas_call x1, Pallas kernels, own_du(): pl.pallas_call(functools.partial(du_kernel, inv_n, n_own), name='own_du',...  51 us
    pallas_call x2, Pallas kernels, put_rows(): pl.pallas_call(copy_kernel, grid_spec=pltpu.PrefetchScalarGridSpec(num_sc...  32.7 us
    pallas_call x1, Pallas kernels, head_grad(): pl.pallas_call(functools.partial(head_grad_kernel, n_own, n_tokens), name...  22.5 us
    pallas_call x1, Pallas kernels, head(): pl.pallas_call(functools.partial(head_kernel, n_masks, window_rows(n_mask...  22.3 us
    ppermute x1, waiting for transfers between devices, local_step(): db2_other = lax.ppermute(db2, 'dp', swap)  17.7 us
  transfers between devices with their start and end apart: 6, of which 3 were waited for; matrix products, arithmetic and copies ran while one was open for 2% of the time, Pallas kernels for 58%

profile of v1, /device:TPU:0, one launch (start us, length us, event | category | flops | bytes accessed | tf_op | source)
XLA Modules:
  0.0 587.1 jit_solution(11455796058900579268)
XLA Ops:
  11.2 22.3 %head.1 = (bf16[928,1024]{1,0:T(8,128)(2,1)S(1)}, f32[928,1024]{1,0:T(8,128)}, bf16[928,1024]{1,0:T(8,128)(2,1)S(1)}, f32[464,1024]{1,0:T(8,128)}) custom-call(s32[1]{0:T(128)} %bitcast.1.vp_ref, s32[928,1]{1,0:T(8,128)S(1)} %pad.71.key_ref, bf16[12,512,1024]{2,1,0:T(8,128)(2,1)} %hidden_ref.1, bf16[1024,1024]{1,0:T(8,128)(2,1)} %w_ref.3, ...), custom_call_target="tpu_custom_call" | custom-call | flops 7784628224 | bytes 12582912 | tf_op jit(solution)/shard_map/head/pallas_call | solution.py:92
  33.5 1.2 copy-done.5
  34.9 56.4 %own_stats.1 = (f32[928,15360]{1,0:T(8,128)}, f32[928,1]{1,0:T(8,128)S(1)}, f32[928,1]{1,0:T(8,128)S(1)}) custom-call(bf16[15296,1024]{1,0:T(8,128)(2,1)} %emb_ref.7, f32[30,1,512]{2,1,0:T(1,128)S(1)} %bitcast.96, bf16[928,1024]{1,0:T(8,128)(2,1)S(1)} %get-tuple-element.29.u_ref), custom_call_target="tpu_custom_call" | custom-call | flops 29192355840 | bytes 57016320 | tf_op jit(solution)/shard_map/own_stats/pallas_call | solution.py:171
  91.8 15.5 %all_gather.13 = f32[256,128]{1,0:T(8,128)S(1)} all-gather(f32[16,128]{1,0:T(8,128)S(1)} %reshape.120), channel_id=1, replica_groups=mesh['vp'=2,'dp'=8] {'vp','dp'}, dimensions={0}, use_global_device_ids=true | all-gather | bytes 139264 | tf_op jit(solution)/shard_map/all_gather | solution.py:479
  109.1 51.0 %own_du.1.du0_ref = f32[928,1024]{1,0:T(8,128)S(1)} custom-call(f32[928,15360]{1,0:T(8,128)} %get-tuple-element.32.logit_ref, bf16[15296,1024]{1,0:T(8,128)(2,1)} %emb_ref.7, s32[30,1,512]{2,1,0:T(1,128)S(1)} %bitcast.95, f32[928,1]{1,0:T(8,128)S(1)} %copy.39.lse_ref, s32[928,1]{1,0:T(8,128)S(1)} %pad.74.lab_ref), custom_call_target="tpu_custom_call" | custom-call | flops 29192355840 | bytes 57016320 | tf_op jit(solution)/shard_map/own_du/pallas_call | solution.py:225
  160.1 1.9 copy-done
  161.9 4.5 copy.40.bias_ref
  166.5 1.0 slice.117
  168.3 16.0 %shard_map.152.u_ref = bf16[7424,1024]{1,0:T(8,128)(2,1)} custom-call(f32[7424,1024]{1,0:T(8,128)} %all-gather.4.cloned.1.call-done.src_ref), custom_call_target="tpu_custom_call" | custom-call | flops 7602176 | bytes 45613056 | tf_op jit(solution)/shard_map/pallas_call | solution.py:420
  184.3 33.9 %shard_map.153 = (f32[768,1024]{1,0:T(8,128)}, f32[768,128]{1,0:T(8,128)}) custom-call(s32[1]{0:T(128)} %bitcast.off_ref, s32[1,7424]{1,0:T(1,128)} %reshape.118.lab_ref, f32[1,7424]{1,0:T(1,128)} %reshape.123.lse_ref, bf16[15296,1024]{1,0:T(8,128)(2,1)} %emb_ref.7, f32[15296,1]{1,0:T(8,128)} %copy.40.bias_ref, bf16[7424,1024]{1,0:T(8,128)(2,1)} %shard_map.152.u_ref), custom_call_target="tpu_custom_call" | custom-call | flops 23353884672 | bytes 19922944 | tf_op jit(solution)/shard_map/pallas_call | solution.py:405
  218.2 1.2 reduce_sum.28
  219.4 4.0 select_maximum_fusion
  223.5 1.5 collective-permute-start
  225.2 83.0 %collective-permute-done.du1_ref = f32[928,1024]{1,0:T(8,128)} collective-permute-done((f32[928,1024]{1,0:T(8,128)}, f32[928,1024]{1,0:T(8,128)}, u32[]{:S(2)}, u32[]{:S(2)}) %collective-permute-start) | collective-permute-done | bytes 3801120 | tf_op jit(solution)/shard_map/ppermute | solution.py:500
  308.1 22.5 %head_grad.1 = (f32[1032,1024]{1,0:T(8,128)}, bf16[928,1024]{1,0:T(8,128)(2,1)}) custom-call(f32[928,1024]{1,0:T(8,128)} %copy-done, f32[928,1024]{1,0:T(8,128)} %collective-permute-done.du1_ref, f32[928,1024]{1,0:T(8,128)} %get-tuple-element.37.pre_ref, bf16[928,1024]{1,0:T(8,128)(2,1)} %copy-done.5, bf16[1024,1024]{1,0:T(8,128)(2,1)} %w_ref.3, ...), custom_call_target="tpu_custom_call" | custom-call | flops 7784628224 | bytes 17104896 | tf_op jit(solution)/shard_map/head_grad/pallas_call | solution.py:285
  330.6 167.6 %shard_map.154 = (f32[4608,1024]{1,0:T(8,128)}, f32[15296,1024]{1,0:T(8,128)}, f32[4608,128]{1,0:T(8,128)}) custom-call(s32[1]{0:T(128)} %bitcast.46.off_ref, s32[1,7424]{1,0:T(1,128)} %reshape.118.lab_ref, f32[1,7424]{1,0:T(1,128)} %reshape.123.lse_ref, bf16[15296,1024]{1,0:T(8,128)(2,1)} %emb_ref.7, f32[15296,1]{1,0:T(8,128)} %copy.40.bias_ref, ...), custom_call_target="tpu_custom_call" | custom-call | flops 140123308032 | bytes 43515904 | tf_op jit(solution)/shard_map/pallas_call | solution.py:405
  500.7 10.6 %scatter.1 = bf16[12,512,1024]{2,1,0:T(8,128)(2,1)} custom-call(s32[12,1,96]{2,1,0:T(1,128)} %broadcast_in_dim.26.pos_ref, bf16[928,1024]{1,0:T(8,128)(2,1)} %get-tuple-element.42.dz_ref), custom_call_target="tpu_custom_call" | custom-call | flops 1207959552 | bytes 12582912 | tf_op jit(solution)/shard_map/scatter/pallas_call | solution.py:315
  511.3 17.7 %collective-permute-done.2 = f32[4608]{0:T(1024)S(1)} collective-permute-done((f32[4608]{0:T(1024)S(1)}, f32[4608]{0:T(1024)S(1)}, u32[]{:S(2)}, u32[]{:S(2)}) %collective-permute-start.2) | collective-permute-done | bytes 18464 | tf_op jit(solution)/shard_map/ppermute | solution.py:507
  530.2 18.6 %shard_map.155.full_ref = f32[15296,1024]{1,0:T(8,128)} custom-call(s32[1]{0:T(128)} %constant.46.clone.1.off_ref, f32[8,776,1024]{2,1,0:T(8,128)} %bitcast.103, f32[15296,1024]{1,0:T(8,128)} %get-tuple-element.46.full_ref), custom_call_target="tpu_custom_call", output_to_operand_aliasing={{}: (2, {})} | custom-call | flops 6291456 | bytes 50331648 | tf_op jit(solution)/shard_map/pallas_call | solution.py:436
  548.8 14.1 %shard_map.156 = f32[15296,1024]{1,0:T(8,128)} custom-call(s32[1]{0:T(128)} %bitcast.45.off_ref, f32[1,4608,1024]{2,1,0:T(8,128)} %bitcast.47.src_ref, f32[15296,1024]{1,0:T(8,128)} %shard_map.155.full_ref), custom_call_target="tpu_custom_call", output_to_operand_aliasing={{}: (2, {})} | custom-call | flops 4718592 | bytes 37748736 | tf_op jit(solution)/shard_map/pallas_call | solution.py:436
  563.5 9.6 %all-reduce.20.cloned.1.call-done = f32[1032,1024]{1,0:T(8,128)} async-done(((f32[1032,1024]{1,0:T(8,128)}), f32[1032,1024]{1,0:T(8,128)}) %all-reduce.20.cloned.1.call-update) | async-done | bytes 4227088 | tf_op jit(solution)/shard_map/psum | solution.py:509
  573.1 4.8 slice.123
  577.9 1.5 fusion.6
  579.4 1.2 slice.122
  (82 shorter events, 11.6 us)
Async XLA Ops:
  7.2 159.3 %all-gather.4.cloned.1.call-start = ((), (), s32[]{:S(2)}) async-start(), calls=%async_computation | async-start | bytes 32309248 | tf_op jit(solution)/shard_map/all_gather | solution.py:468
  9.2 0.7 copy-start.1
  9.9 0.7 copy-start.2
  10.5 0.7 copy-start.3
  11.2 23.6 %copy-start.7 = (f32[15296]{0:T(1024)S(1)}, f32[15296]{0:T(1024)}, u32[]{:S(2)}) copy-start(f32[15296]{0:T(1024)} %param.17) | copy-start | bytes 183556
  33.5 1.2 copy-start.5
  34.8 463.5 %all-gather.6.cloned.1.call-start = ((), (), s32[]{:S(2)}) async-start(), calls=%async_computation.2 | async-start | bytes 28606464 | tf_op jit(solution)/shard_map/all_gather | solution.py:498
  160.1 1.9 copy-start
  219.4 88.7 %copy-start.4 = (f32[1024]{0:T(1024)S(1)}, f32[1024]{0:T(1024)}, u32[]{:S(2)}) copy-start(f32[1024]{0:T(1024)} %param.14) | copy-start | bytes 12292
  223.4 349.7 %all-reduce.20.cloned.1.call-start = ((), (), s32[]{:S(2)}) async-start(), calls=%async_computation.1 | async-start | bytes 8454144 | tf_op jit(solution)/shard_map/psum | solution.py:509
  223.5 84.7 %collective-permute-start = (f32[928,1024]{1,0:T(8,128)}, f32[928,1024]{1,0:T(8,128)}, u32[]{:S(2)}, u32[]{:S(2)}) collective-permute-start(f32[928,1024]{1,0:T(8,128)} %copy-done), channel_id=1, source_target_pairs={{0,8},{8,0},{1,9},{9,1},{2,10},{10,2},{3,11},{11,3},{4,12},{12,4},... | collective-permute-start | bytes 11403272 | tf_op jit(solution)/shard_map/ppermute | solution.py:500
  498.2 0.7 copy-start.8
  498.2 1.8 copy-start.6
  498.2 50.6 %collective-permute-start.1 = (f32[4608,1024]{1,0:T(8,128)}, f32[4608,1024]{1,0:T(8,128)}, u32[]{:S(2)}, u32[]{:S(2)}) collective-permute-start(f32[4608,1024]{1,0:T(8,128)} %get-tuple-element.44), channel_id=1, source_target_pairs={{0,1},{1,0},{2,3},{3,2},{4,5},{5,4},{6,7},{7,6},{8,9},{9,8},{10,11... | collective-permute-start | bytes 56623112 | tf_op jit(solution)/shard_map/ppermute | solution.py:505
  500.7 28.3 %collective-permute-start.2 = (f32[4608]{0:T(1024)S(1)}, f32[4608]{0:T(1024)S(1)}, u32[]{:S(2)}, u32[]{:S(2)}) collective-permute-start(f32[4608]{0:T(1024)S(1)} %reduce_sum.29), channel_id=1, source_target_pairs={{0,1},{1,0},{2,3},{3,2},{4,5},{5,4},{6,7},{7,6},{8,9},{9,8},{10,11... | collective-permute-start | bytes 55304 | tf_op jit(solution)/shard_map/ppermute | solution.py:507
Sparse Core Ops, SparseCore 0:
  34.9 124.3 all-gather.3
  223.5 122.7 all-gather.5
  498.4 74.6 all-reduce.19

commit v2 on v1

--- a/solution.py
+++ b/solution.py
@@ -15,11 +15,12 @@
 NT = (((1,), (1,)), ((), ()))
 LANES = 128
 SUBLANES = 16
-ROWS = 32
+ROWS = 128
 NEGATIVE = -1e30
 OWN_V = 512
 TILE_V = 768
 TILE_T = 512
+FINISH_TILES = 2
 GATHERED_TILES = 1
 
 
@@ -36,10 +37,12 @@
 
 def row_loop(rows, step, body):
     def run(i, carry):
-        body(pl.multiple_of(i * step, step))
+        body(pl.multiple_of(i * step, step), step)
         return carry
 
     lax.fori_loop(0, rows // step, run, 0)
+    if rows % step:
+        body(rows - rows % step, rows % step)
 
 
 def window_start(n_masks, c):
@@ -66,8 +69,8 @@
         z_ref[...] = z_acc[...].astype(BF16)
         pre_ref[...] = jnp.dot(z_ref[...], w_ref[...], preferred_element_type=F32) + b_ref[...]
 
-        def norm(r):
-            at = pl.ds(r, ROWS)
+        def norm(r, count):
+            at = pl.ds(r, count)
             _, g = gelu_parts(pre_ref[at, :])
             xhat, _ = normalised(g)
             u = xhat * gain_ref[...] + beta_ref[...]
@@ -110,8 +113,7 @@
     )(vp, key, hidden, w, b.reshape(1, width), gain.reshape(1, width), beta.reshape(1, width), label_row)
 
 
-def row_blocks(rows):
-    n = 4
+def row_blocks(rows, n):
     sixteenths = rows // SUBLANES
     sizes = [(sixteenths // n + (i < sixteenths % n)) * SUBLANES for i in range(n)]
     return [slice(sum(sizes[:i]), sum(sizes[: i + 1])) for i in range(n)]
@@ -125,7 +127,7 @@
         m_acc[...] = jnp.full_like(m_acc, NEGATIVE)
         l_acc[...] = jnp.zeros_like(l_acc)
 
-    blocks = row_blocks(u_ref.shape[0])
+    blocks = row_blocks(u_ref.shape[0], 2)
 
     def logits(rows):
         logit_ref[rows, :] = lax.dot_general(u_ref[rows, :], emb_ref[...], NT, preferred_element_type=F32) + bias_ref[...]
@@ -187,7 +189,7 @@
 
 def du_kernel(inv_n, spare, logit_ref, emb_ref, ids_ref, lse_ref, lab_ref, du_ref, lse_b, lab_b, hit_acc, acc):
     i = pl.program_id(0)
-    blocks = row_blocks(lse_ref.shape[0])
+    blocks = row_blocks(lse_ref.shape[0], 2)
 
     @pl.when(i == 0)
     def _():
@@ -247,11 +249,11 @@
         a[...] = jnp.zeros_like(a)
 
     def fold(x):
-        return functools.reduce(jnp.add, [x[8 * j : 8 * (j + 1), :] for j in range(ROWS // 8)])
-
-    def body(r):
-        at = pl.ds(r, ROWS)
-        real = r + lax.broadcasted_iota(jnp.int32, (ROWS, width), 0) < n_own
+        return functools.reduce(jnp.add, [x[8 * j : 8 * (j + 1), :] for j in range(x.shape[0] // 8)])
+
+    def body(r, count):
+        at = pl.ds(r, count)
+        real = r + lax.broadcasted_iota(jnp.int32, (count, width), 0) < n_own
         du = jnp.where(real, du0_ref[at, :] + du1_ref[at, :], 0.0)
         a = pre_ref[at, :]
         cdf, g = gelu_parts(a)
@@ -323,71 +325,232 @@
     )(pos[:, None, :], dz)
 
 
-def emb_grad_kernel(tc, n, tail, inv_n, bv, off_ref, lab_ref, lse_ref, emb_ref, bias_ref, u_ref, *rest):
-    (*dout_refs, db_ref, s0, s1, bb_ref) = rest
-    acc = dout_refs[0]
-    row0 = (off_ref[0] + pl.program_id(0)) * bv
-    bb_ref[...] = jnp.broadcast_to(bias_ref[...], (bv, LANES))
-    db_ref[...] = jnp.zeros_like(db_ref)
-    acc[...] = jnp.zeros_like(acc)
+def emb_grad_kernel(tc, n, tail, inv_n, bv, grid_tiles, mode, *refs):
+    off_ref, lab_ref, lse_ref, emb_ref, bias_ref, u_hbm, *rest = refs
+    if mode == "first":
+        out_ref, u_out, u_ref, s0, s1, bb_ref, db_acc, in_sem, stage, out_sem = rest
+    elif mode == "place":
+        acc, db_ref, full_ref, u_ref, s0, s1, bb_ref, db_acc, in_sem = rest
+    else:
+        rows1, rows2, _, acc, db_ref, full_ref, u_ref, s0, s1, bb_ref, db_acc, in_sem, cbuf, cin_sem, cout_sem, put_sem = rest
+    if mode == "first":
+        acc, db_ref = out_ref.at[pl.ds(0, bv), :], out_ref.at[pl.ds(bv, 1), pl.ds(0, bv)]
+    step = pl.program_id(0)
+    tile = off_ref[0] + step
+    row0 = tile * bv
+    last = n + (1 if tail else 0)
 
     def at(i):
         return i * tc if isinstance(i, int) else pl.multiple_of(i * tc, tc)
 
-    def dot1(t0, w):
-        return lax.dot_general(emb_ref[...], u_ref[pl.ds(t0, w), :], NT, preferred_element_type=F32)
-
-    def grad(s_ref, t0, w):
+    def size(i):
+        return tail if isinstance(i, int) and i == n else tc
+
+    def fetch(i):
+        slot = stage.at[i % 4 if isinstance(i, int) else lax.rem(i, 4)] if mode == "first" else u_ref.at[pl.ds(at(i), size(i)), :]
+        if mode == "first" and size(i) != tc:
+            slot = slot.at[pl.ds(0, size(i)), :]
+        return pltpu.make_async_copy(u_hbm.at[pl.ds(at(i), size(i)), :], slot, in_sem.at[i])
+
+    def hand_on(i):
+        here = pl.ds(at(i), size(i))
+        return pltpu.make_async_copy(u_ref.at[here, :], u_out.at[here, :], out_sem.at[i])
+
+    def arrive(i):
+        fetch(i).wait()
+
+    def rounded(i):
+        slot = i % 4 if isinstance(i, int) else lax.rem(i, 4)
+        u_ref[pl.ds(at(i), size(i)), :] = stage[slot, : size(i), :].astype(BF16)
+
+    def dot1(i):
+        return lax.dot_general(emb_ref[...], u_ref[pl.ds(at(i), size(i)), :], NT, preferred_element_type=F32)
+
+    def grad(s_ref, i):
         ids = row0 + lax.broadcasted_iota(jnp.int32, (bv, LANES), 0)
         total = None
         parts = []
-        for j in range(w // LANES):
-            cols = pl.ds(t0 + LANES * j, LANES)
+        for j in range(size(i) // LANES):
+            cols = pl.ds(at(i) + LANES * j, LANES)
             x = s_ref[:, LANES * j : LANES * (j + 1)] + bb_ref[...] - lse_ref[:, cols]
             g = jnp.exp(x) - jnp.where(ids == lab_ref[:, cols], inv_n, 0.0)
             total = g if total is None else total + g
             parts.append(g.astype(BF16))
-        db_ref[...] += total
+        db_acc[...] += total
         return jnp.concatenate(parts, axis=1)
 
-    def dot2(g, t0, w):
-        acc[...] += jnp.dot(g, u_ref[pl.ds(t0, w), :], preferred_element_type=F32)
-
-    s0[...] = dot1(0, tc)
+    def dot2(s_ref, i):
+        acc[...] += jnp.dot(grad(s_ref, i), u_ref[pl.ds(at(i), size(i)), :], preferred_element_type=F32)
+
+    if mode == "first":
+        for i in range(4):
+            fetch(i).start()
+    else:
+
+        @pl.when(step == 0)
+        def _():
+            for i in range(last):
+                fetch(i).start()
+
+    bb_ref[...] = jnp.broadcast_to(bias_ref[...], (LANES, bv)).T
+    db_acc[...] = jnp.zeros_like(db_acc)
+    acc[...] = jnp.zeros_like(acc)
+
+    def need(*chunks):
+        if mode != "first":
+
+            @pl.when(step == 0)
+            def _():
+                for i in chunks:
+                    arrive(i)
+
+    if mode == "first":
+        for i in range(3):
+            arrive(i)
+            rounded(i)
+            if i + 4 < last:
+                fetch(i + 4).start()
+    need(0)
+    s0[...] = dot1(0)
+    if mode == "first":
+        hand_on(0).start()
+
+    def two_chunks(a):
+        if mode == "first":
+            for i in (a + 3, a + 4):
+                arrive(i)
+            for i in (a + 1, a + 2):
+                hand_on(i).start()
+        elif mode == "finish":
+            copy_blocks(step * (n // 2 - 1) + a // 2)
+        need(a + 1, a + 2)
+        s1[...] = dot1(a + 1)
+        dot2(s0, a)
+        if mode == "first":
+            for i in (a + 3, a + 4):
+                rounded(i)
+        s0[...] = dot1(a + 2)
+        dot2(s1, a + 1)
+        if mode == "first":
+            for i in (a + 7, a + 8):
+                if isinstance(i, int):
+                    if i < last:
+                        fetch(i).start()
+                else:
+                    full_chunks = i < n
+                    pl.when(full_chunks)(lambda i=i: fetch(i).start())
+                    if tail:
+                        pl.when(i == n)(lambda: fetch(n).start())
+
+    def copy_blocks(t):
+        n1, n2 = rows1.shape[0], rows2.shape[0] // bv
+        t = jnp.int32(t)
+        slot, other = lax.rem(t, 2), 1 - lax.rem(t, 2)
+        put = lambda x, where: pltpu.make_async_copy(cbuf.at[x], full_ref.at[pl.ds(where, bv), :], cout_sem.at[x])
+        take1 = lambda x, b: pltpu.make_async_copy(rows1.at[b, pl.ds(0, bv), :], cbuf.at[x], cin_sem.at[x])
+        take2 = lambda x, b: pltpu.make_async_copy(rows2.at[pl.ds(pl.multiple_of(b * bv, bv), bv), :], cbuf.at[x], cin_sem.at[x])
+
+        @pl.when((t >= 2) & (t < n1 + n2 + 2))
+        def _():
+            put(slot, 0).wait()
+
+        @pl.when(t < n1)
+        def _():
+            take1(slot, t).start()
+
+        @pl.when((t >= n1) & (t < n1 + n2))
+        def _():
+            take2(slot, t - n1).start()
+
+        @pl.when((t >= 1) & (t < n1 + n2 + 1))
+        def _():
+            take1(other, 0).wait()
+            where = jnp.where(t <= n1, t - 1, off_ref[1] + t - 1 - n1) * bv
+            put(other, pl.multiple_of(where, bv)).start()
 
     def body(i, carry):
-        a = 2 * i
-        s1[...] = dot1(at(a + 1), tc)
-        dot2(grad(s0, at(a), tc), at(a), tc)
-        s0[...] = dot1(at(a + 2), tc)
-        dot2(grad(s1, at(a + 1), tc), at(a + 1), tc)
+        two_chunks(2 * i)
         return carry
 
-    lax.fori_loop(0, n // 2 - 1, body, 0)
-    s1[...] = dot1((n - 1) * tc, tc)
-    dot2(grad(s0, (n - 2) * tc, tc), (n - 2) * tc, tc)
+    trips = n // 2 - 1
+    if mode == "first":
+        lax.fori_loop(0, trips - 1, body, 0)
+        two_chunks(2 * (trips - 1))
+    else:
+        lax.fori_loop(0, trips, body, 0)
+    if mode == "first":
+        for i in range(n - 1, last):
+            hand_on(i).start()
+    need(*range(n - 1, last))
+    s1[...] = dot1(n - 1)
+    dot2(s0, n - 2)
     if tail:
-        s0[:, :tail] = dot1(n * tc, tail)
-    dot2(grad(s1, (n - 1) * tc, tc), (n - 1) * tc, tc)
+        s0[:, :tail] = dot1(n)
+    dot2(s1, n - 1)
     if tail:
-        dot2(grad(s0, n * tc, tail), n * tc, tail)
-    for other in dout_refs[1:]:
-        other[...] = acc[...]
-
-
-def emb_grad(first_tile, n_tiles, place_rows, inv_n, labels, lse, emb, bias, u):
+        dot2(s0, n)
+
+    db_ref[...] = jnp.sum(db_acc[...].T, axis=0, keepdims=True)
+    if mode == "first":
+        for i in range(last):
+            hand_on(i).wait()
+    elif mode == "place":
+        full_ref[...] = acc[...]
+    else:
+        rows = full_ref.shape[0]
+        whole, part = rows // bv, rows % bv
+
+        def put_tile(count):
+            copy = pltpu.make_async_copy(acc.at[pl.ds(0, count), :], full_ref.at[pl.ds(pl.multiple_of(row0, bv), count), :], put_sem)
+            copy.start()
+            copy.wait()
+
+        pl.when(tile < whole)(lambda: put_tile(bv))
+        if part:
+            pl.when(tile == whole)(lambda: put_tile(part))
+
+        @pl.when(step == pl.num_programs(0) - 1)
+        def _():
+            for t in range(grid_tiles * trips, rows1.shape[0] + rows2.shape[0] // bv + 2):
+                copy_blocks(t)
+
+
+def emb_grad(mode, tiles, n_tiles, inv_n, labels, lse, emb, bias, u, *moved):
     n_tok, width = u.shape
     n, tail = divmod(n_tok, TILE_T)
     if n % 2:
         n, tail = n - 1, tail + TILE_T
+    chunks = n + (1 if tail else 0)
     bv = TILE_V
     rows = n_tiles * bv
     once = pl.Buffered(1)
-    out_specs = [pl.BlockSpec((bv, width), lambda i, o: (i, 0)), pl.BlockSpec((bv, LANES), lambda i, o: (i, 0))]
-    out_shape = [jax.ShapeDtypeStruct((rows, width), F32), jax.ShapeDtypeStruct((rows, LANES), F32)]
-    if place_rows:
-        out_specs.insert(1, pl.BlockSpec((bv, width), lambda i, o: (o[0] + i, 0)))
-        out_shape.insert(1, jax.ShapeDtypeStruct((place_rows, width), F32))
+    anywhere = pl.BlockSpec(memory_space=pl.ANY)
+    full = jax.ShapeDtypeStruct(emb.shape, F32)
+    extra = 8 if mode == "first" else 0
+    out_specs = [pl.BlockSpec((bv + extra, width), lambda i, o: (i, 0))]
+    out_shape = [jax.ShapeDtypeStruct((n_tiles * (bv + extra), width), F32)]
+    if mode != "first":
+        out_specs.append(pl.BlockSpec((None, 1, bv), lambda i, o: (i, 0, 0)))
+        out_shape.append(jax.ShapeDtypeStruct((n_tiles, 1, bv), F32))
+    scratch = [
+        pltpu.VMEM((n_tok, width), BF16),
+        pltpu.VMEM((bv, TILE_T), F32),
+        pltpu.VMEM((bv, TILE_T), F32),
+        pltpu.VMEM((bv, LANES), F32),
+        pltpu.VMEM((bv, LANES), F32),
+        pltpu.SemaphoreType.DMA((chunks,)),
+    ]
+    if mode == "first":
+        out_specs.append(anywhere)
+        out_shape.append(jax.ShapeDtypeStruct(u.shape, BF16))
+        scratch += [pltpu.VMEM((4, TILE_T, width), F32), pltpu.SemaphoreType.DMA((chunks,))]
+    elif mode == "place":
+        out_specs.append(pl.BlockSpec((bv, width), lambda i, o: (o[0] + i, 0)))
+        out_shape.append(full)
+    else:
+        out_specs.append(anywhere)
+        out_shape.append(full)
+        scratch += [pltpu.VMEM((2, bv, width), F32), pltpu.SemaphoreType.DMA((2,)), pltpu.SemaphoreType.DMA((2,)), pltpu.SemaphoreType.DMA]
     grid_spec = pltpu.PrefetchScalarGridSpec(
         num_scalar_prefetch=1,
         grid=(n_tiles,),
@@ -395,36 +558,21 @@
             pl.BlockSpec((1, n_tok), lambda i, o: (0, 0), pipeline_mode=once),
             pl.BlockSpec((1, n_tok), lambda i, o: (0, 0), pipeline_mode=once),
             pl.BlockSpec((bv, width), lambda i, o: (o[0] + i, 0)),
-            pl.BlockSpec((bv, 1), lambda i, o: (o[0] + i, 0)),
-            pl.BlockSpec((n_tok, width), lambda i, o: (0, 0), pipeline_mode=once),
-        ],
+            pl.BlockSpec((1, bv), lambda i, o: (0, o[0] + i)),
+        ]
+        + [anywhere] * (1 + len(moved)),
         out_specs=out_specs,
-        scratch_shapes=[pltpu.VMEM((bv, TILE_T), F32), pltpu.VMEM((bv, TILE_T), F32), pltpu.VMEM((bv, LANES), F32)],
+        scratch_shapes=scratch,
     )
     flops = 4 * rows * n_tok * width
     return pl.pallas_call(
-        functools.partial(emb_grad_kernel, TILE_T, n, tail, inv_n, bv),
+        functools.partial(emb_grad_kernel, TILE_T, n, tail, inv_n, bv, n_tiles, mode),
         grid_spec=grid_spec,
         out_shape=out_shape,
+        input_output_aliases={8: 2} if mode == "finish" else {},
         compiler_params=pltpu.CompilerParams(vmem_limit_bytes=62_000_000),
         cost_estimate=pl.CostEstimate(flops=flops, bytes_accessed=n_tok * width * 2 + rows * width * 6, transcendentals=rows * n_tok),
-    )(first_tile, labels, lse, emb, bias, u)
-
-
-def round_kernel(src_ref, out_ref):
-    out_ref[...] = src_ref[...].astype(out_ref.dtype)
-
-
-def round_rows(src, block):
-    rows, width = src.shape
-    return pl.pallas_call(
-        round_kernel,
-        grid=(rows // block,),
-        in_specs=[pl.BlockSpec((block, width), lambda i: (i, 0))],
-        out_specs=pl.BlockSpec((block, width), lambda i: (i, 0)),
-        out_shape=jax.ShapeDtypeStruct(src.shape, BF16),
-        cost_estimate=pl.CostEstimate(flops=rows * width, bytes_accessed=rows * width * 6, transcendentals=0),
-    )(src)
+    )(tiles, labels, lse, emb, bias, u, *moved)
 
 
 def copy_kernel(off_ref, src_ref, full_ref, out_ref):
@@ -466,7 +614,6 @@
         label_row = jnp.pad(labels.reshape(1, n_own).astype(F32), ((0, 0), (0, width - n_own)), constant_values=-1.0)
         z, pre_act, u_own, sent = head(vp.reshape(1), mask_pos, hidden, w_trans, b_trans, ln_gain, ln_bias, label_row, slots, half)
         gathered = lax.all_gather(sent, ("vp", "dp"), axis=0, tiled=True)
-        u_all = round_rows(gathered, slots)
 
         def token_order(rows):
             return jnp.swapaxes(rows.reshape(n_groups, n_vp, half), 0, 1).reshape(1, -1)
@@ -490,31 +637,36 @@
         k = GATHERED_TILES
         m = (tiles - n_groups * k) // 2
         core = lax.rem(me, 2)
-        bias_col = b_vocab.reshape(shard_rows, 1)
+        bias_row = b_vocab.reshape(1, shard_rows)
         lse_all, du_part = lax.optimization_barrier((lse_all, du_part))
-        part1, db1 = emb_grad((me * k).reshape(1), k, 0, 1.0 / n_tokens, labels_all, lse_all, emb_table, bias_col, u_all)
-        mine = (n_groups * k + core * m).reshape(1)
-        theirs = (n_groups * k + (1 - core) * m).reshape(1)
-        rows1 = lax.all_gather(jnp.concatenate([part1, jnp.pad(jnp.pad(jnp.sum(db1, axis=1), (0, -k * TILE_V % width)).reshape(-1, width), ((0, 8 - pl.cdiv(k * TILE_V, width)), (0, 0)))]), "dp", axis=0)
+        pair = lambda a, b: jnp.stack([a, b]).astype(jnp.int32)
+        part1, u_all = emb_grad("first", pair(me * k, 0), k, 1.0 / n_tokens, labels_all, lse_all, emb_table, bias_row, gathered)
+        du_other = lax.ppermute(du_part, "vp", [(0, 1), (1, 0)])
+        rows1 = lax.all_gather(part1, "dp", axis=0)
+
         swap = [(i, i ^ 1) for i in range(n_groups)]
-        du_other = lax.ppermute(du_part, "vp", [(0, 1), (1, 0)])
+        mb = FINISH_TILES
+        ma = m - mb
+        mine = n_groups * k + core * m
+        theirs = n_groups * k + (1 - core) * m
+        part2a, db2a, full = emb_grad("place", pair(mine, theirs), ma, 1.0 / n_tokens, labels_all, lse_all, emb_table, bias_row, u_all)
+        rows2a = lax.ppermute(part2a, "dp", swap)
+
+        du_other, db2a = lax.optimization_barrier((du_other, db2a))
         sum_in, dz = head_grad(du_part, du_other, pre_act, z, w_trans, ln_gain, norm_own, n_own, n_tokens)
-        lse_all, sum_in = lax.optimization_barrier((lse_all, sum_in))
-
-        part2, full, db2 = emb_grad(mine, m, shard_rows, 1.0 / n_tokens, labels_all, lse_all, emb_table, bias_col, u_all)
-        rows2 = lax.ppermute(part2, "dp", swap)
-        db2 = jnp.sum(db2, axis=1)
+        sums = lax.psum(sum_in, "dp")
+
+        lse_last, sum_in = lax.optimization_barrier((lse_all, sum_in))
+        part2b, db2b, full = emb_grad("finish", pair(mine + ma, theirs), mb, 1.0 / n_tokens, labels_all, lse_last, emb_table, bias_row, u_all, rows1, rows2a, full)
+        rows2b = lax.ppermute(part2b, "dp", swap)
+        db2 = jnp.concatenate([db2a, db2b]).reshape(-1)
         db2_other = lax.ppermute(db2, "dp", swap)
-        rows1, sum_in = lax.optimization_barrier((rows1, sum_in))
-        sums = lax.psum(sum_in, "dp")
-
-        full = put_rows(jnp.zeros((1,), jnp.int32), rows1, full, n_groups, k)
-        d_emb_table = put_rows(theirs, rows2[None], full, 1, m)
-        db1_all = rows1[:, k * TILE_V :].reshape(n_groups, -1)[:, : k * TILE_V].reshape(-1)
+        dz, db2 = lax.optimization_barrier((dz, db2))
+        d_hidden = scatter(mask_pos, dz, seq_len)
+        d_emb_table = put_rows((theirs + ma).reshape(1), rows2b[None], full, 1, mb)
+        db1_all = rows1.reshape(n_groups * k, TILE_V + 8, width)[:, TILE_V, :TILE_V].reshape(-1)
         db_first, db_last = jnp.where(core == 0, db2, db2_other), jnp.where(core == 0, db2_other, db2)
         d_b_vocab = jnp.concatenate([db1_all, db_first, db_last])[:shard_rows]
-
-        d_hidden = scatter(mask_pos, dz, seq_len)
         return sums[width + 3, 0], d_hidden, sums[:width], sums[width], sums[width + 1], sums[width + 2], d_emb_table, d_b_vocab
 
     in_specs = (P("dp", None, None), P("dp", None), P("dp", None), P(None, None), P(None), P(None), P(None), P("vp", None), P("vp"))

time: 590 us -> 580 us (0.983)
  Pallas kernels: 413 us -> 363 us
  waiting for transfers between devices: 110 us -> 155 us
    psum x1, waiting for transfers between devices: 9.6 us -> 73.5 us  [local_step(): sums = lax.psum(sum_in, 'dp')]
    pallas_call x2 -> x1, Pallas kernels: 32.7 us -> 4.71 us  [put_rows(): pl.pallas_call(copy_kernel, grid_spec=pltpu.PrefetchScalarGridSpec(num_sc...]
    ppermute x1, waiting for transfers between devices: 17.7 us -> 0.01 us  [local_step(): db2_other = lax.ppermute(db2, 'dp', swap)]
    pallas_call x1 -> x0, Pallas kernels: 16 us -> none  [round_rows(): pl.pallas_call(round_kernel, grid=(rows // block,), in_specs=[pl.BlockSpe...]
    pallas_call x1, Pallas kernels: 22.5 us -> 15.3 us  [head_grad(): pl.pallas_call(functools.partial(head_grad_kernel, n_own, n_tokens), name...]
    pallas_call x2 -> x3, Pallas kernels: 201 us -> 208 us  [emb_grad(): pl.pallas_call(functools.partial(emb_grad_kernel, TILE_T, n, tail, inv_n,...]
  transfers between devices with their start and end apart: 6 -> 7, of which waited for: 3 -> 2; matrix products, arithmetic and copies ran while one was open for 2% -> 3% of each run, Pallas kernels for 58% -> 42%
where the time goes in v2:
time: 580 us; the launch traced here: 573 us
  Pallas kernels  363 us (63%)
  waiting for transfers between devices  155 us (27%)
  local copies, waits for them, and re-layouts  18.6 us (3%)
  blocking collectives  15.5 us (3%)
  between operations  14.4 us (2%)
    pallas_call x3, Pallas kernels, emb_grad(): pl.pallas_call(functools.partial(emb_grad_kernel, TILE_T, n, tail, inv_n,...  208 us
    ppermute x1, waiting for transfers between devices, local_step(): du_other = lax.ppermute(du_part, 'vp', [(0, 1), (1, 0)])  81.1 us
    psum x1, waiting for transfers between devices, local_step(): sums = lax.psum(sum_in, 'dp')  73.5 us
    pallas_call x1, Pallas kernels, own_stats(): pl.pallas_call(stats_kernel, name='own_stats', grid=(n,), in_specs=[tile_...  54 us
    pallas_call x1, Pallas kernels, own_du(): pl.pallas_call(functools.partial(du_kernel, inv_n, n_own), name='own_du',...  52 us
    pallas_call x1, Pallas kernels, head(): pl.pallas_call(functools.partial(head_kernel, n_masks, window_rows(n_mask...  18.3 us
    all_gather x1, blocking collectives, local_step(): lax.all_gather(stats, ('vp', 'dp'), axis=0, tiled=True)  15.5 us
    pallas_call x1, Pallas kernels, head_grad(): pl.pallas_call(functools.partial(head_grad_kernel, n_own, n_tokens), name...  15.3 us
  transfers between devices with their start and end apart: 7, of which 2 were waited for; matrix products, arithmetic and copies ran while one was open for 3% of the time, Pallas kernels for 42%

profile of v2, /device:TPU:0, one launch (start us, length us, event | category | flops | bytes accessed | tf_op | source)
XLA Modules:
  0.0 573.3 jit_solution(15731703564195972581)
XLA Ops:
  7.2 0.8 broadcast_subtract_fusion
  8.1 0.8 broadcast_add_fusion
  11.2 18.3 %head.1 = (bf16[928,1024]{1,0:T(8,128)(2,1)S(1)}, f32[928,1024]{1,0:T(8,128)}, bf16[928,1024]{1,0:T(8,128)(2,1)S(1)}, f32[464,1024]{1,0:T(8,128)}) custom-call(s32[1]{0:T(128)} %bitcast.1.vp_ref, s32[928,1]{1,0:T(8,128)S(1)} %pad.63.key_ref, bf16[12,512,1024]{2,1,0:T(8,128)(2,1)} %hidden_ref.1, bf16[1024,1024]{1,0:T(8,128)(2,1)} %w_ref.3, ...), custom_call_target="tpu_custom_call" | custom-call | flops 7784628224 | bytes 12582912 | tf_op jit(solution)/shard_map/head/pallas_call | solution.py:95
  29.5 1.3 copy-done.4
  31.0 54.0 %own_stats.1 = (f32[928,15360]{1,0:T(8,128)}, f32[928,1]{1,0:T(8,128)S(1)}, f32[928,1]{1,0:T(8,128)S(1)}) custom-call(bf16[15296,1024]{1,0:T(8,128)(2,1)} %refs_3_.5, f32[30,1,512]{2,1,0:T(1,128)S(1)} %bitcast.95, bf16[928,1024]{1,0:T(8,128)(2,1)S(1)} %get-tuple-element.32.u_ref), custom_call_target="tpu_custom_call" | custom-call | flops 29192355840 | bytes 57016320 | tf_op jit(solution)/shard_map/own_stats/pallas_call | solution.py:173
  85.5 15.5 %all_gather.12 = f32[256,128]{1,0:T(8,128)S(1)} all-gather(f32[16,128]{1,0:T(8,128)S(1)} %reshape.105), channel_id=1, replica_groups=mesh['vp'=2,'dp'=8] {'vp','dp'}, dimensions={0}, use_global_device_ids=true | all-gather | bytes 139264 | tf_op jit(solution)/shard_map/all_gather | solution.py:626
  102.5 0.7 reshape.108.refs_2_
  103.4 52.0 %own_du.1.du0_ref = f32[928,1024]{1,0:T(8,128)} custom-call(f32[928,15360]{1,0:T(8,128)} %get-tuple-element.35.logit_ref, bf16[15296,1024]{1,0:T(8,128)(2,1)} %refs_3_.5, s32[30,1,512]{2,1,0:T(1,128)S(1)} %bitcast.94, f32[928,1]{1,0:T(8,128)S(1)} %copy.35.lse_ref, s32[928,1]{1,0:T(8,128)S(1)} %pad.66.lab_ref), custom_call_target="tpu_custom_call" | custom-call | flops 29192355840 | bytes 57016320 | tf_op jit(solution)/shard_map/own_du/pallas_call | solution.py:227
  156.0 1.0 slice.117
  157.1 0.7 reshape.113.refs_1_
  157.8 34.1 %shard_map.152 = (f32[776,1024]{1,0:T(8,128)}, bf16[7424,1024]{1,0:T(8,128)(2,1)}) custom-call(s32[2]{0:T(128)} %pad_add_fusion.1.refs_0_, s32[1,7424]{1,0:T(1,128)} %reshape.113.refs_1_, f32[1,7424]{1,0:T(1,128)} %reshape.108.refs_2_, bf16[15296,1024]{1,0:T(8,128)(2,1)} %refs_3_.5, f32[1,15296]{1,0:T(1,128)} %bitcast.103, ...), custom_call_target="tpu_custom_call" | custom-call | flops 23353884672 | bytes 19922944 | tf_op jit(solution)/shard_map/pallas_call | solution.py:568
  192.6 110.8 %shard_map.153 = (f32[3072,1024]{1,0:T(8,128)}, f32[4,1,768]{2,1,0:T(1,128)}, f32[15296,1024]{1,0:T(8,128)}) custom-call(s32[2]{0:T(128)} %pad_add_fusion.refs_0_, s32[1,7424]{1,0:T(1,128)} %reshape.113.refs_1_, f32[1,7424]{1,0:T(1,128)} %reshape.108.refs_2_, bf16[15296,1024]{1,0:T(8,128)(2,1)} %refs_3_.5, f32[1,15296]{1,0:T(1,128)} %bitcast.104, ...), custom_call_target="tpu_custom_call" | custom-call | flops 93415538688 | bytes 34078720 | tf_op jit(solution)/shard_map/pallas_call | solution.py:568
  303.9 1.9 collective-permute-start
  305.8 0.8 dynamic-slice_bitcast_fusion
  307.4 81.1 %collective-permute-done.du1_ref = f32[928,1024]{1,0:T(8,128)} collective-permute-done((f32[928,1024]{1,0:T(8,128)}, f32[928,1024]{1,0:T(8,128)}, u32[]{:S(2)}, u32[]{:S(2)}) %collective-permute-start) | collective-permute-done | bytes 3801120 | tf_op jit(solution)/shard_map/ppermute | solution.py:644
  388.5 15.3 %head_grad.1 = (f32[1032,1024]{1,0:T(8,128)}, bf16[928,1024]{1,0:T(8,128)(2,1)}) custom-call(f32[928,1024]{1,0:T(8,128)} %own_du.1.du0_ref, f32[928,1024]{1,0:T(8,128)} %collective-permute-done.du1_ref, f32[928,1024]{1,0:T(8,128)} %get-tuple-element.42.pre_ref, bf16[928,1024]{1,0:T(8,128)(2,1)} %copy-done.4, bf16[1024,1024]{1,0:T(8,128)(2,1)} %w_ref.3, ...), custom_call_target="tpu_custom_call" | custom-call | flops 7784628224 | bytes 17104896 | tf_op jit(solution)/shard_map/head_grad/pallas_call | solution.py:287
  403.9 63.4 %shard_map.154 = (f32[1536,1024]{1,0:T(8,128)}, f32[2,1,768]{2,1,0:T(1,128)}, f32[15296,1024]{1,0:T(8,128)}) custom-call(s32[2]{0:T(128)} %pad_add_fusion.2.refs_0_, s32[1,7424]{1,0:T(1,128)} %reshape.113.refs_1_, f32[1,7424]{1,0:T(1,128)} %reshape.108.refs_2_, bf16[15296,1024]{1,0:T(8,128)(2,1)} %refs_3_.5, ...), custom_call_target="tpu_custom_call", output_to_operand_aliasing={{2}: (8, {})} | custom-call | flops 46707769344 | bytes 24641536 | tf_op jit(solution)/shard_map/pallas_call | solution.py:568
  468.5 73.5 %all-reduce.18.cloned.1.call-done = f32[1032,1024]{1,0:T(8,128)} async-done(((f32[1032,1024]{1,0:T(8,128)}), f32[1032,1024]{1,0:T(8,128)}) %all-reduce.18.cloned.1.call-update) | async-done | bytes 4227088 | tf_op jit(solution)/shard_map/psum | solution.py:657
  542.0 4.8 slice.119
  546.8 1.2 slice.118
  548.0 1.5 fusion.6
  549.6 10.6 %scatter.1 = bf16[12,512,1024]{2,1,0:T(8,128)(2,1)} custom-call(s32[12,1,96]{2,1,0:T(1,128)} %broadcast_in_dim.26.pos_ref, bf16[928,1024]{1,0:T(8,128)(2,1)} %get-tuple-element.52.dz_ref), custom_call_target="tpu_custom_call" | custom-call | flops 1207959552 | bytes 12582912 | tf_op jit(solution)/shard_map/scatter/pallas_call | solution.py:317
  560.2 0.9 slice.123
  561.8 4.7 shard_map.155
  (82 shorter events, 9.2 us)
Async XLA Ops:
  7.2 148.8 %all-gather.4.cloned.1.call-start = ((), (), s32[]{:S(2)}) async-start(), calls=%async_computation | async-start | bytes 32309248 | tf_op jit(solution)/shard_map/all_gather | solution.py:616
  9.2 0.7 copy-start
  9.9 0.7 copy-start.1
  10.5 0.7 copy-start.2
  11.2 19.7 %copy-start.6 = (f32[15296]{0:T(1024)S(1)}, f32[15296]{0:T(1024)}, u32[]{:S(2)}) copy-start(f32[15296]{0:T(1024)} %param.17) | copy-start | bytes 183556
  29.5 1.3 copy-start.4
  30.9 373.0 %all-gather.6.cloned.1.call-start = ((), (), s32[]{:S(2)}) async-start(), calls=%async_computation.2 | async-start | bytes 28606464 | tf_op jit(solution)/shard_map/all_gather | solution.py:645
  101.3 0.6 copy-start.5
  191.9 350.1 %all-reduce.18.cloned.1.call-start = ((), (), s32[]{:S(2)}) async-start(), calls=%async_computation.1 | async-start | bytes 8454144 | tf_op jit(solution)/shard_map/psum | solution.py:657
  192.6 195.9 %copy-start.3 = (f32[1024]{0:T(1024)S(1)}, f32[1024]{0:T(1024)}, u32[]{:S(2)}) copy-start(f32[1024]{0:T(1024)} %param.14) | copy-start | bytes 12292
  303.4 100.5 %collective-permute-start.1 = (f32[3072,1024]{1,0:T(8,128)}, f32[3072,1024]{1,0:T(8,128)}, u32[]{:S(2)}, u32[]{:S(2)}) collective-permute-start(f32[3072,1024]{1,0:T(8,128)} %get-tuple-element.49), channel_id=1, source_target_pairs={{0,1},{1,0},{2,3},{3,2},{4,5},{5,4},{6,7},{7,6},{8,9},{9,8},{10,11... | collective-permute-start | bytes 37748744 | tf_op jit(solution)/shard_map/ppermute | solution.py:653
  303.9 84.6 %collective-permute-start = (f32[928,1024]{1,0:T(8,128)}, f32[928,1024]{1,0:T(8,128)}, u32[]{:S(2)}, u32[]{:S(2)}) collective-permute-start(f32[928,1024]{1,0:T(8,128)} %own_du.1.du0_ref), channel_id=1, source_target_pairs={{0,8},{8,0},{1,9},{9,1},{2,10},{10,2},{3,11},{11,3},{4,12},{12,4},... | collective-permute-start | bytes 11403272 | tf_op jit(solution)/shard_map/ppermute | solution.py:644
  403.9 63.5 %copy-start.7 = (s32[12,77]{1,0:T(8,128)S(1)}, s32[12,77]{1,0:T(8,128)}, u32[]{:S(2)}) copy-start(s32[12,77]{1,0:T(8,128)} %param.10) | copy-start | bytes 11092
  467.2 82.2 %copy-start.8 = (f32[4,1,768]{2,1,0:T(1,128)S(1)}, f32[4,1,768]{2,1,0:T(1,128)}, u32[]{:S(2)}) copy-start(f32[4,1,768]{2,1,0:T(1,128)} %get-tuple-element.46) | copy-start | bytes 36868
  467.3 82.2 %copy-start.9 = (f32[2,1,768]{2,1,0:T(1,128)S(1)}, f32[2,1,768]{2,1,0:T(1,128)}, u32[]{:S(2)}) copy-start(f32[2,1,768]{2,1,0:T(1,128)} %get-tuple-element.51) | copy-start | bytes 18436
  467.3 94.5 %collective-permute-start.2 = (f32[1536,1024]{1,0:T(8,128)}, f32[1536,1024]{1,0:T(8,128)}, u32[]{:S(2)}, u32[]{:S(2)}) collective-permute-start(f32[1536,1024]{1,0:T(8,128)} %get-tuple-element.53), channel_id=1, source_target_pairs={{0,1},{1,0},{2,3},{3,2},{4,5},{5,4},{6,7},{7,6},{8,9},{9,8},{10,11... | collective-permute-start | bytes 18874376 | tf_op jit(solution)/shard_map/ppermute | solution.py:661
  549.6 11.6 %collective-permute-start.3 = (f32[4608]{0:T(1024)S(1)}, f32[4608]{0:T(1024)S(1)}, u32[]{:S(2)}, u32[]{:S(2)}) collective-permute-start(f32[4608]{0:T(1024)S(1)} %reshape.116), channel_id=1, source_target_pairs={{0,1},{1,0},{2,3},{3,2},{4,5},{5,4},{6,7},{7,6},{8,9},{9,8},{10,11... | collective-permute-start | bytes 55304 | tf_op jit(solution)/shard_map/ppermute | solution.py:663
Sparse Core Ops, SparseCore 0:
  31.0 124.2 all-gather.3
  192.1 124.7 all-gather.5
  467.5 74.5 all-reduce.17

commit v3 on v2

--- a/solution.py
+++ b/solution.py
@@ -16,6 +16,7 @@
 LANES = 128
 SUBLANES = 16
 ROWS = 128
+GROUP = 2
 NEGATIVE = -1e30
 OWN_V = 512
 TILE_V = 768
@@ -49,31 +50,33 @@
     return pl.multiple_of(n_masks * c // SUBLANES * SUBLANES, SUBLANES)
 
 
-def head_kernel(n_masks, window, label_at, vp_ref, key_ref, hidden_ref, w_ref, b_ref, gain_ref, beta_ref, label_ref,
+def head_kernel(n_masks, window, label_at, vp_ref, key_ref, hidden_ref, w_ref, rows_ref,
                 z_ref, pre_ref, u_ref, sent_ref, z_acc, u_acc):
     c = pl.program_id(0)
-    slots, seq_len = z_ref.shape[0], hidden_ref.shape[0]
+    slots, (group, seq_len, _) = z_ref.shape[0], hidden_ref.shape
     half = sent_ref.shape[0]
 
     @pl.when(c == 0)
     def _():
         z_acc[...] = jnp.zeros_like(z_acc)
 
-    here = pl.ds(window_start(n_masks, c), window)
-    ids = c * seq_len + lax.broadcasted_iota(jnp.int32, (window, seq_len), 1)
-    pick = (key_ref[here, :] == ids).astype(F32).astype(BF16)
-    z_acc[here, :] += jnp.dot(pick, hidden_ref[...], preferred_element_type=F32)
+    for q in range(group):
+        row = c * group + q
+        here = pl.ds(window_start(n_masks, row), window)
+        ids = row * seq_len + lax.broadcasted_iota(jnp.int32, (window, seq_len), 1)
+        pick = (key_ref[here, :] == ids).astype(F32).astype(BF16)
+        z_acc[here, :] += jnp.dot(pick, hidden_ref[q], preferred_element_type=F32)
 
     @pl.when(c == pl.num_programs(0) - 1)
     def _():
         z_ref[...] = z_acc[...].astype(BF16)
-        pre_ref[...] = jnp.dot(z_ref[...], w_ref[...], preferred_element_type=F32) + b_ref[...]
+        pre_ref[...] = jnp.dot(z_ref[...], w_ref[...], preferred_element_type=F32) + rows_ref[0:1, :]
 
         def norm(r, count):
             at = pl.ds(r, count)
             _, g = gelu_parts(pre_ref[at, :])
             xhat, _ = normalised(g)
-            u = xhat * gain_ref[...] + beta_ref[...]
+            u = xhat * rows_ref[1:2, :] + rows_ref[2:3, :]
             u_acc[at, :] = u
             u_ref[at, :] = u.astype(BF16)
 
@@ -82,7 +85,7 @@
 
         @pl.when(vp_ref[0] == label_at // half)
         def _():
-            sent_ref[label_at % half : label_at % half + 1, :] = label_ref[...]
+            sent_ref[label_at % half : label_at % half + 1, :] = rows_ref[3:4, :]
 
 
 def head(vp, mask_pos, hidden, w, b, gain, beta, label_row, slots, half):
@@ -97,8 +100,8 @@
         name="head",
         grid_spec=pltpu.PrefetchScalarGridSpec(
             num_scalar_prefetch=1,
-            grid=(n_rows,),
-            in_specs=[whole(slots, 1), pl.BlockSpec((None, seq_len, width), lambda c, v: (c, 0, 0)), whole(width, width)] + [whole(1, width)] * 4,
+            grid=(n_rows // GROUP,),
+            in_specs=[whole(slots, 1), pl.BlockSpec((GROUP, seq_len, width), lambda c, v: (c, 0, 0)), whole(width, width), whole(4, width)],
             out_specs=[out(slots), out(slots), out(slots), out(half)],
             scratch_shapes=[pltpu.VMEM((slots, width), F32), pltpu.VMEM((slots, width), F32)],
         ),
@@ -110,7 +113,7 @@
         ],
         compiler_params=pltpu.CompilerParams(vmem_limit_bytes=50_000_000),
         cost_estimate=pl.CostEstimate(flops=2 * slots * width * width * 4, bytes_accessed=hidden.size * 2, transcendentals=slots * width),
-    )(vp, key, hidden, w, b.reshape(1, width), gain.reshape(1, width), beta.reshape(1, width), label_row)
+    )(vp, key, hidden, w, jnp.concatenate([b[None], gain[None], beta[None], label_row]))
 
 
 def row_blocks(rows, n):
@@ -301,11 +304,12 @@
 
 
 def scatter_kernel(n_masks, window, pos_ref, dz_ref, out_ref):
-    c = pl.program_id(0)
-    seq_len = out_ref.shape[0]
-    hit = pos_ref[...] == lax.broadcasted_iota(jnp.int32, (seq_len, window), 0)
-    rows = dz_ref[pl.ds(window_start(n_masks, c), window), :]
-    out_ref[...] = jnp.dot(hit.astype(F32).astype(BF16), rows, preferred_element_type=F32).astype(BF16)
+    group, seq_len, _ = out_ref.shape
+    for q in range(group):
+        row = pl.program_id(0) * group + q
+        hit = pos_ref[q] == lax.broadcasted_iota(jnp.int32, (seq_len, window), 0)
+        rows = dz_ref[pl.ds(window_start(n_masks, row), window), :]
+        out_ref[q] = jnp.dot(hit.astype(F32).astype(BF16), rows, preferred_element_type=F32).astype(BF16)
 
 
 def scatter(mask_pos, dz, seq_len):
@@ -317,9 +321,9 @@
     return pl.pallas_call(
         functools.partial(scatter_kernel, n_masks, window),
         name="scatter",
-        grid=(n_rows,),
-        in_specs=[pl.BlockSpec((None, 1, window), lambda c: (c, 0, 0)), pl.BlockSpec(dz.shape, lambda c: (0, 0), pipeline_mode=pl.Buffered(1))],
-        out_specs=pl.BlockSpec((None, seq_len, width), lambda c: (c, 0, 0)),
+        grid=(n_rows // GROUP,),
+        in_specs=[pl.BlockSpec((GROUP, 1, window), lambda c: (c, 0, 0)), pl.BlockSpec(dz.shape, lambda c: (0, 0), pipeline_mode=pl.Buffered(1))],
+        out_specs=pl.BlockSpec((GROUP, seq_len, width), lambda c: (c, 0, 0)),
         out_shape=jax.ShapeDtypeStruct((n_rows, seq_len, width), BF16),
         cost_estimate=pl.CostEstimate(flops=2 * n_rows * seq_len * window * width, bytes_accessed=n_rows * seq_len * width * 2, transcendentals=0),
     )(pos[:, None, :], dz)
@@ -656,13 +660,12 @@
         sum_in, dz = head_grad(du_part, du_other, pre_act, z, w_trans, ln_gain, norm_own, n_own, n_tokens)
         sums = lax.psum(sum_in, "dp")
 
-        lse_last, sum_in = lax.optimization_barrier((lse_all, sum_in))
+        d_hidden = scatter(mask_pos, dz, seq_len)
+        lse_last, d_hidden = lax.optimization_barrier((lse_all, d_hidden))
         part2b, db2b, full = emb_grad("finish", pair(mine + ma, theirs), mb, 1.0 / n_tokens, labels_all, lse_last, emb_table, bias_row, u_all, rows1, rows2a, full)
         rows2b = lax.ppermute(part2b, "dp", swap)
         db2 = jnp.concatenate([db2a, db2b]).reshape(-1)
         db2_other = lax.ppermute(db2, "dp", swap)
-        dz, db2 = lax.optimization_barrier((dz, db2))
-        d_hidden = scatter(mask_pos, dz, seq_len)
         d_emb_table = put_rows((theirs + ma).reshape(1), rows2b[None], full, 1, mb)
         db1_all = rows1.reshape(n_groups * k, TILE_V + 8, width)[:, TILE_V, :TILE_V].reshape(-1)
         db_first, db_last = jnp.where(core == 0, db2, db2_other), jnp.where(core == 0, db2_other, db2)

time: 580 us -> 573 us (0.988)
  Pallas kernels: 363 us -> 356 us
where the time goes in v3:
time: 573 us; the launch traced here: 566 us
  Pallas kernels  356 us (62%)
  waiting for transfers between devices  153 us (27%)
  local copies, waits for them, and re-layouts  18.3 us (3%)
  blocking collectives  15.5 us (3%)
  between operations  14.3 us (2%)
    pallas_call x3, Pallas kernels, emb_grad(): pl.pallas_call(functools.partial(emb_grad_kernel, TILE_T, n, tail, inv_n,...  208 us
    ppermute x1, waiting for transfers between devices, local_step(): du_other = lax.ppermute(du_part, 'vp', [(0, 1), (1, 0)])  80 us
    psum x1, waiting for transfers between devices, local_step(): sums = lax.psum(sum_in, 'dp')  73.3 us
    pallas_call x1, Pallas kernels, own_stats(): pl.pallas_call(stats_kernel, name='own_stats', grid=(n,), in_specs=[tile_...  54 us
    pallas_call x1, Pallas kernels, own_du(): pl.pallas_call(functools.partial(du_kernel, inv_n, n_own), name='own_du',...  50.1 us
    all_gather x1, blocking collectives, local_step(): lax.all_gather(stats, ('vp', 'dp'), axis=0, tiled=True)  15.5 us
    pallas_call x1, Pallas kernels, head_grad(): pl.pallas_call(functools.partial(head_grad_kernel, n_own, n_tokens), name...  15.5 us
    pallas_call x1, Pallas kernels, head(): pl.pallas_call(functools.partial(head_kernel, n_masks, window_rows(n_mask...  15.2 us
  transfers between devices with their start and end apart: 7, of which 2 were waited for; matrix products, arithmetic and copies ran while one was open for 3% of the time, Pallas kernels for 42%

profile of v3, /device:TPU:0, one launch (start us, length us, event | category | flops | bytes accessed | tf_op | source)
XLA Modules:
  0.0 566.4 jit_solution(2800370287212084033)
XLA Ops:
  7.2 0.8 broadcast_add_fusion
  8.2 0.8 broadcast_subtract_fusion
  9.9 15.2 %head.1 = (bf16[928,1024]{1,0:T(8,128)(2,1)S(1)}, f32[928,1024]{1,0:T(8,128)}, bf16[928,1024]{1,0:T(8,128)(2,1)S(1)}, f32[464,1024]{1,0:T(8,128)}) custom-call(s32[1]{0:T(128)} %bitcast.1.vp_ref, s32[928,1]{1,0:T(8,128)S(1)} %pad.63.key_ref, bf16[12,512,1024]{2,1,0:T(8,128)(2,1)} %hidden_ref.1, bf16[1024,1024]{1,0:T(8,128)(2,1)} %w_ref.3, ...), custom_call_target="tpu_custom_call" | custom-call | flops 7784628224 | bytes 12582912 | tf_op jit(solution)/shard_map/head/pallas_call | solution.py:98
  25.1 1.3 copy-done.2
  26.6 54.0 %own_stats.1 = (f32[928,15360]{1,0:T(8,128)}, f32[928,1]{1,0:T(8,128)S(1)}, f32[928,1]{1,0:T(8,128)S(1)}) custom-call(bf16[15296,1024]{1,0:T(8,128)(2,1)} %refs_3_.5, f32[30,1,512]{2,1,0:T(1,128)S(1)} %bitcast.95, bf16[928,1024]{1,0:T(8,128)(2,1)S(1)} %get-tuple-element.31.u_ref), custom_call_target="tpu_custom_call" | custom-call | flops 29192355840 | bytes 57016320 | tf_op jit(solution)/shard_map/own_stats/pallas_call | solution.py:176
  81.0 15.5 %all_gather.12 = f32[256,128]{1,0:T(8,128)S(1)} all-gather(f32[16,128]{1,0:T(8,128)S(1)} %reshape.93), channel_id=1, replica_groups=mesh['vp'=2,'dp'=8] {'vp','dp'}, dimensions={0}, use_global_device_ids=true | all-gather | bytes 139264 | tf_op jit(solution)/shard_map/all_gather | solution.py:630
  99.0 50.1 %own_du.1.du0_ref = f32[928,1024]{1,0:T(8,128)S(1)} custom-call(f32[928,15360]{1,0:T(8,128)} %get-tuple-element.34.logit_ref, bf16[15296,1024]{1,0:T(8,128)(2,1)} %refs_3_.5, s32[30,1,512]{2,1,0:T(1,128)S(1)} %bitcast.94, f32[928,1]{1,0:T(8,128)S(1)} %copy.35.lse_ref, s32[928,1]{1,0:T(8,128)S(1)} %pad.66.lab_ref), custom_call_target="tpu_custom_call" | custom-call | flops 29192355840 | bytes 57016320 | tf_op jit(solution)/shard_map/own_du/pallas_call | solution.py:230
  149.1 1.9 copy-done.1
  151.6 1.0 slice.117
  153.4 34.0 %shard_map.152 = (f32[776,1024]{1,0:T(8,128)}, bf16[7424,1024]{1,0:T(8,128)(2,1)}) custom-call(s32[2]{0:T(128)} %pad_add_fusion.1.refs_0_, s32[1,7424]{1,0:T(1,128)} %reshape.101.refs_1_, f32[1,7424]{1,0:T(1,128)} %reshape.96.refs_2_, bf16[15296,1024]{1,0:T(8,128)(2,1)} %refs_3_.5, f32[1,15296]{1,0:T(1,128)} %bitcast.101, ...), custom_call_target="tpu_custom_call" | custom-call | flops 23353884672 | bytes 19922944 | tf_op jit(solution)/shard_map/pallas_call | solution.py:572
  188.1 110.8 %shard_map.153 = (f32[3072,1024]{1,0:T(8,128)}, f32[4,1,768]{2,1,0:T(1,128)}, f32[15296,1024]{1,0:T(8,128)}) custom-call(s32[2]{0:T(128)} %pad_add_fusion.refs_0_, s32[1,7424]{1,0:T(1,128)} %reshape.101.refs_1_, f32[1,7424]{1,0:T(1,128)} %reshape.96.refs_2_, bf16[15296,1024]{1,0:T(8,128)(2,1)} %refs_3_.5, f32[1,15296]{1,0:T(1,128)} %bitcast.102, ...), custom_call_target="tpu_custom_call" | custom-call | flops 93415538688 | bytes 34078720 | tf_op jit(solution)/shard_map/pallas_call | solution.py:572
  299.4 1.9 collective-permute-start
  301.3 0.8 dynamic-slice_bitcast_fusion
  304.0 80.0 %collective-permute-done.du1_ref = f32[928,1024]{1,0:T(8,128)} collective-permute-done((f32[928,1024]{1,0:T(8,128)}, f32[928,1024]{1,0:T(8,128)}, u32[]{:S(2)}, u32[]{:S(2)}) %collective-permute-start) | collective-permute-done | bytes 3801120 | tf_op jit(solution)/shard_map/ppermute | solution.py:648
  384.0 15.5 %head_grad.1 = (f32[1032,1024]{1,0:T(8,128)}, bf16[928,1024]{1,0:T(8,128)(2,1)}) custom-call(f32[928,1024]{1,0:T(8,128)} %copy-done.1, f32[928,1024]{1,0:T(8,128)} %collective-permute-done.du1_ref, f32[928,1024]{1,0:T(8,128)} %get-tuple-element.41.pre_ref, bf16[928,1024]{1,0:T(8,128)(2,1)} %copy-done.2, bf16[1024,1024]{1,0:T(8,128)(2,1)} %w_ref.3, ...), custom_call_target="tpu_custom_call" | custom-call | flops 7784628224 | bytes 17104896 | tf_op jit(solution)/shard_map/head_grad/pallas_call | solution.py:290
  399.5 8.5 %scatter.1 = bf16[12,512,1024]{2,1,0:T(8,128)(2,1)} custom-call(s32[12,1,96]{2,1,0:T(1,128)} %broadcast_in_dim.38.pos_ref, bf16[928,1024]{1,0:T(8,128)(2,1)} %get-tuple-element.44.dz_ref), custom_call_target="tpu_custom_call" | custom-call | flops 1207959552 | bytes 12582912 | tf_op jit(solution)/shard_map/scatter/pallas_call | solution.py:321
  408.0 63.2 %shard_map.154 = (f32[1536,1024]{1,0:T(8,128)}, f32[2,1,768]{2,1,0:T(1,128)}, f32[15296,1024]{1,0:T(8,128)}) custom-call(s32[2]{0:T(128)} %pad_add_fusion.2.refs_0_, s32[1,7424]{1,0:T(1,128)} %reshape.101.refs_1_, f32[1,7424]{1,0:T(1,128)} %reshape.96.refs_2_, bf16[15296,1024]{1,0:T(8,128)(2,1)} %refs_3_.5, ...), custom_call_target="tpu_custom_call", output_to_operand_aliasing={{2}: (8, {})} | custom-call | flops 46707769344 | bytes 24641536 | tf_op jit(solution)/shard_map/pallas_call | solution.py:572
  471.3 0.7 maximum_reduce_fusion
  472.6 73.3 %all-reduce.18.cloned.1.call-done = f32[1032,1024]{1,0:T(8,128)} async-done(((f32[1032,1024]{1,0:T(8,128)}), f32[1032,1024]{1,0:T(8,128)}) %all-reduce.18.cloned.1.call-update) | async-done | bytes 4227088 | tf_op jit(solution)/shard_map/psum | solution.py:661
  545.9 1.5 fusion.6
  547.4 1.2 slice.118
  548.6 4.8 slice.119
  553.4 0.9 slice.123
  555.0 4.7 shard_map.155
  (76 shorter events, 9.7 us)
Async XLA Ops:
  7.2 144.4 %all-gather.4.cloned.1.call-start = ((), (), s32[]{:S(2)}) async-start(), calls=%async_computation | async-start | bytes 32309248 | tf_op jit(solution)/shard_map/all_gather | solution.py:620
  9.9 16.6 %copy-start.4 = (f32[15296]{0:T(1024)S(1)}, f32[15296]{0:T(1024)}, u32[]{:S(2)}) copy-start(f32[15296]{0:T(1024)} %param.17) | copy-start | bytes 183556
  25.1 1.3 copy-start.2
  26.4 381.6 %all-gather.6.cloned.1.call-start = ((), (), s32[]{:S(2)}) async-start(), calls=%async_computation.2 | async-start | bytes 28606464 | tf_op jit(solution)/shard_map/all_gather | solution.py:649
  96.9 0.6 copy-start.3
  149.1 1.9 copy-start.1
  187.5 358.4 %all-reduce.18.cloned.1.call-start = ((), (), s32[]{:S(2)}) async-start(), calls=%async_computation.1 | async-start | bytes 8454144 | tf_op jit(solution)/shard_map/psum | solution.py:661
  188.1 114.2 %copy-start.5 = (s32[12,77]{1,0:T(8,128)S(1)}, s32[12,77]{1,0:T(8,128)}, u32[]{:S(2)}) copy-start(s32[12,77]{1,0:T(8,128)} %param.10) | copy-start | bytes 11092
  188.1 195.9 %copy-start = (f32[1024]{0:T(1024)S(1)}, f32[1024]{0:T(1024)}, u32[]{:S(2)}) copy-start(f32[1024]{0:T(1024)} %param.14) | copy-start | bytes 12292
  298.9 109.1 %collective-permute-start.1 = (f32[3072,1024]{1,0:T(8,128)}, f32[3072,1024]{1,0:T(8,128)}, u32[]{:S(2)}, u32[]{:S(2)}) collective-permute-start(f32[3072,1024]{1,0:T(8,128)} %get-tuple-element.48), channel_id=1, source_target_pairs={{0,1},{1,0},{2,3},{3,2},{4,5},{5,4},{6,7},{7,6},{8,9},{9,8},{10,11... | collective-permute-start | bytes 37748744 | tf_op jit(solution)/shard_map/ppermute | solution.py:657
  299.4 84.6 %collective-permute-start = (f32[928,1024]{1,0:T(8,128)}, f32[928,1024]{1,0:T(8,128)}, u32[]{:S(2)}, u32[]{:S(2)}) collective-permute-start(f32[928,1024]{1,0:T(8,128)} %copy-done.1), channel_id=1, source_target_pairs={{0,8},{8,0},{1,9},{9,1},{2,10},{10,2},{3,11},{11,3},{4,12},{12,4},... | collective-permute-start | bytes 11403272 | tf_op jit(solution)/shard_map/ppermute | solution.py:648
  408.0 63.3 %copy-start.6 = (f32[4,1,768]{2,1,0:T(1,128)S(1)}, f32[4,1,768]{2,1,0:T(1,128)}, u32[]{:S(2)}) copy-start(f32[4,1,768]{2,1,0:T(1,128)} %get-tuple-element.52) | copy-start | bytes 36868
  471.2 83.7 %collective-permute-start.2 = (f32[1536,1024]{1,0:T(8,128)}, f32[1536,1024]{1,0:T(8,128)}, u32[]{:S(2)}, u32[]{:S(2)}) collective-permute-start(f32[1536,1024]{1,0:T(8,128)} %get-tuple-element.50), channel_id=1, source_target_pairs={{0,1},{1,0},{2,3},{3,2},{4,5},{5,4},{6,7},{7,6},{8,9},{9,8},{10,11... | collective-permute-start | bytes 18874376 | tf_op jit(solution)/shard_map/ppermute | solution.py:666
  472.1 82.2 %collective-permute-start.3 = (f32[4608]{0:T(1024)S(1)}, f32[4608]{0:T(1024)S(1)}, u32[]{:S(2)}, u32[]{:S(2)}) collective-permute-start(f32[4608]{0:T(1024)S(1)} %reshape.105), channel_id=1, source_target_pairs={{0,1},{1,0},{2,3},{3,2},{4,5},{5,4},{6,7},{7,6},{8,9},{9,8},{10,11... | collective-permute-start | bytes 55304 | tf_op jit(solution)/shard_map/ppermute | solution.py:668
Sparse Core Ops, SparseCore 0:
  26.5 124.2 all-gather.3
  187.6 124.6 all-gather.5
  471.4 74.4 all-reduce.17
